TPU v7x, 128 devices: a whole 4x4x4 slice. The times are simulated.
128 devices in a mesh: lat: 16 (over y, z), ch: 8 (over x, core).
Axes of the slice: x: 4, y: 4, z: 4, core: 2. Of those that a mesh axis runs over, the one named last changes fastest.
Arguments:
- field_in: bfloat16 [768, 384, 768], P('ch', 'lat'), may hold values from -80 to 80
- ln_gain: float32 [2, 768], P(None, 'ch'), may hold values from 0.5 to 1.5
- ln_shift: float32 [2, 768], P(None, 'ch'), may hold values from -1.5 to 1.5
- mix_first: bfloat16 [2, 2, 8, 96, 96], P(None, None, 'ch'), may hold values from -0.4375 to 0.4375
- mix_bias: bfloat16 [2, 2, 8, 96], P(None, None, 'ch'), may hold values from -3 to 3
- mix_second: bfloat16 [2, 2, 8, 96, 96], P(None, None, 'ch'), may hold values from -0.4375 to 0.4375
Outputs:
- field_out: bfloat16 [768, 384, 768], P('ch', 'lat')
All inputs are finite; a program needn't handle non-finite values.
Results may differ from a plain program's by a relative error of at most 0.014.
Values may be sent and summed in bfloat16 or wider, within the bound.
A program may use at most 128 MiB of HBM per device.

v0:
```python
import functools
import math

import jax
import jax.numpy as jnp
from jax import lax
from jax.sharding import Mesh
from jax.sharding import PartitionSpec as P

CH = ("ch_0", "ch_1")
LAT = ("lat_0", "lat_1")
LAT_CH = ("lat_0", "lat_1", "ch_0", "ch_1")


norm_eps = 1e-05
shrink_level = 0.01


def copy_for_each(x, axis):
    copies = jnp.broadcast_to(x, (lax.axis_size(axis), *x.shape))
    return lax.all_to_all(copies, axis, split_axis=0, concat_axis=0, tiled=True)


def taken_together(x, axis):
    everything = copy_for_each(x, axis)
    return jnp.sum(everything.astype(jnp.float32), axis=0)


def by_axis(x, axes):
    return functools.reduce(lax.psum, axes, x)


def soft_shrink(values):
    return jnp.sign(values) * jnp.maximum(jnp.abs(values) - shrink_level, 0.0)


def trig_angles(length, freq_ids):
    positions = jnp.arange(length, dtype=jnp.int32)
    phase_ids = positions[:, None] * freq_ids[None, :] % length
    angles = phase_ids.astype(jnp.float32) * (2.0 * math.pi / length)
    norm_scale = 1.0 / math.sqrt(length)
    return (jnp.cos(angles) * norm_scale, jnp.sin(angles) * norm_scale)


def lon_tables(lon_cells, pieces):
    mode_count = lon_cells // 2
    per_piece = mode_count // pieces
    column = jnp.arange(2 * mode_count, dtype=jnp.int32)
    is_imag = column // per_piece % 2
    freq_ids = column // (2 * per_piece) * per_piece + column % per_piece
    cos_part, sin_part = trig_angles(lon_cells, freq_ids)
    forward = jnp.where(is_imag[None, :] == 0, cos_part, -sin_part).astype(jnp.bfloat16)
    weight_k = jnp.where(freq_ids == 0, 1.0, 2.0).astype(jnp.float32)
    inverse = (forward.astype(jnp.float32).T * weight_k[:, None]).astype(jnp.bfloat16)
    return (forward, inverse)


def normalize(source, gain, shift):
    ch_all = source.shape[0] * lax.axis_size(CH)
    total_sum, squares = (
        taken_together(jnp.sum(source, axis=0).astype(jnp.bfloat16), CH).astype(jnp.float32),
        taken_together(jnp.sum(source * source, axis=0).astype(jnp.bfloat16), CH).astype(
            jnp.float32
        ),
    )
    mean_val = total_sum / ch_all
    spread = squares / ch_all - mean_val * mean_val
    inv_std = lax.rsqrt(spread + norm_eps)
    gain_col = gain[:, None, None]
    shift_col = shift[:, None, None]
    return ((source - mean_val) * inv_std * gain_col + shift_col).astype(jnp.bfloat16)


def lat_transform(mode_data, cos_lat, sin_lat, backward):
    chans, lat_rows, width_q = mode_data.shape
    part_cos = jnp.einsum("hj,chq->cjq", cos_lat, mode_data, preferred_element_type=jnp.float32)
    part_sin = jnp.einsum("hj,chq->cjq", sin_lat, mode_data, preferred_element_type=jnp.float32)
    part_cos = part_cos.reshape(chans, lat_rows, 2, width_q // 2)
    part_sin = part_sin.reshape(chans, lat_rows, 2, width_q // 2)
    if backward:
        real_part = part_cos[:, :, 0] - part_sin[:, :, 1]
        imag_part = part_cos[:, :, 1] + part_sin[:, :, 0]
    else:
        real_part = part_cos[:, :, 0] + part_sin[:, :, 1]
        imag_part = part_cos[:, :, 1] - part_sin[:, :, 0]
    return jnp.stack([real_part, imag_part], axis=2).astype(jnp.bfloat16)


def contract(operand, weight):
    return jnp.einsum("bcjm,bcd->bdjm", operand, weight, preferred_element_type=jnp.float32)


def block_mix(lat_spec, first_w, first_b, second_w, block_width):
    chans, lat_rows, two_parts, per_piece = lat_spec.shape
    block_count = chans // block_width
    grouped = lat_spec.reshape(block_count, block_width, lat_rows, two_parts, per_piece)
    spec_re = grouped[:, :, :, 0]
    spec_im = grouped[:, :, :, 1]
    bias_f = first_b.astype(jnp.float32)
    hid_re = jax.nn.relu(
        contract(spec_re, first_w[0]) - contract(spec_im, first_w[1]) + bias_f[0][:, :, None, None]
    ).astype(jnp.bfloat16)
    hid_im = jax.nn.relu(
        contract(spec_im, first_w[0]) + contract(spec_re, first_w[1]) + bias_f[1][:, :, None, None]
    ).astype(jnp.bfloat16)
    mix_re = soft_shrink(contract(hid_re, second_w[0]) - contract(hid_im, second_w[1])).astype(
        jnp.bfloat16
    )
    mix_im = soft_shrink(contract(hid_im, second_w[0]) + contract(hid_re, second_w[1])).astype(
        jnp.bfloat16
    )
    return jnp.stack([mix_re, mix_im], axis=3).reshape(chans, lat_rows, two_parts * per_piece)


def per_device(field_in, ln_gain, ln_shift, mix_first, mix_bias, mix_second):
    lat_parts = lax.axis_size(LAT)
    ch_dev, band_rows, lon_cells = field_in.shape
    lat_rows = band_rows * lat_parts
    block_width = mix_first.shape[-1]
    first_all, bias_all, second_all = (mix_first, mix_bias, mix_second)
    per_piece = lon_cells // 2 // lat_parts
    forward, inverse = lon_tables(lon_cells, lat_parts)
    cos_f, sin_f = trig_angles(lat_rows, jnp.arange(lat_rows, dtype=jnp.int32))
    cos_lat = cos_f.astype(jnp.bfloat16)
    sin_lat = sin_f.astype(jnp.bfloat16)
    row_pos = (lax.axis_index(LAT) * band_rows + jnp.arange(band_rows, dtype=jnp.int32)).astype(
        jnp.float32
    )
    area_weights = jnp.cos((row_pos + 0.5) * (math.pi / lat_rows) - 0.5 * math.pi)[None, :, None]
    source = field_in.astype(jnp.float32)
    target = by_axis(jnp.sum(area_weights * source * source), LAT_CH)
    current = field_in
    for layer_idx in range(mix_first.shape[0]):
        normed = normalize(source, ln_gain[layer_idx], ln_shift[layer_idx])
        lon_spec = jnp.dot(
            normed.reshape(ch_dev * band_rows, lon_cells),
            forward,
            preferred_element_type=jnp.float32,
        ).astype(jnp.bfloat16)
        mode_data = lax.all_to_all(
            lon_spec.reshape(ch_dev, band_rows, lon_cells),
            LAT,
            split_axis=2,
            concat_axis=1,
            tiled=True,
        )
        lat_spec = lat_transform(mode_data, cos_lat, sin_lat, False)
        mixed_spec = block_mix(
            lat_spec, first_all[layer_idx], bias_all[layer_idx], second_all[layer_idx], block_width
        )
        back_spec = lat_transform(mixed_spec, cos_lat, sin_lat, True).reshape(
            ch_dev, lat_rows, 2 * per_piece
        )
        band_spec = lax.all_to_all(back_spec, LAT, split_axis=1, concat_axis=2, tiled=True)
        spatial = jnp.dot(
            band_spec.reshape(ch_dev * band_rows, lon_cells),
            inverse,
            preferred_element_type=jnp.float32,
        )
        spatial = spatial.reshape(ch_dev, band_rows, lon_cells)
        summed = spatial + normed.astype(jnp.float32) + current.astype(jnp.float32)
        energy = by_axis(jnp.sum(area_weights * summed * summed), LAT_CH)
        current = (summed * jnp.sqrt(target / energy)).astype(jnp.bfloat16)
        source = current.astype(jnp.float32)
    return current


def solution(mesh):
    finer = Mesh(mesh.devices.reshape(4, 4, 4, 2), ("lat_0", "lat_1", "ch_0", "ch_1"))
    in_specs = (
        P(CH, LAT, None),
        P(None, CH),
        P(None, CH),
        P(None, None, CH, None, None),
        P(None, None, CH, None),
        P(None, None, CH, None, None),
    )
    out_specs = P(CH, LAT, None)
    return jax.shard_map(
        per_device, mesh=finer, in_specs=in_specs, out_specs=out_specs, check_vma=False
    )
```

profile of v0, /device:TPU:1, one launch (start us, length us, event | category | flops | bytes accessed | tf_op | source)
XLA Modules:
  0.0 625.2 jit_solution(16360192033380045489)
XLA Ops:
  4.8 5.8 all-to-all-start
  11.9 5.5 all-to-all-done
  19.0 5.0 all-to-all-start.1
  26.8 4.1 all-to-all-done.1
  34.2 15.9 %convolution_convert_fusion.1 = bf16[2304,768]{1,0:T(8,128)(2,1)} fusion(bf16[2304,768]{1,0:T(8,128)(2,1)S(1)} %bitcast.246, s32[768]{0:T(1024)S(1)} %copy-done.12, pred[768]{0:T(1024)(128)(4,1)S(1)} %copy-done.21), kind=kOutput, calls=%fused_computation.26 | convolution fusion | flops 2727936000 | bytes 7081728 | tf_op jit(solution)/shard_map/dot_general | solution.py:135
  50.2 7.1 %copy.99 = bf16[96,24,768]{0,1,2:T(8,128)(2,1)} copy(bf16[96,24,768]{2,1,0:T(8,128)(2,1)} %bitcast.244) | data formatting | bytes 7077888 | tf_op jit(solution)/shard_map/reshape | solution.py:141
  57.3 7.8 %all-to-all-start.2 = ((bf16[96,24,768]{0,1,2:T(8,128)(2,1)}), bf16[96,24,768]{0,1,2:T(8,128)(2,1)}, u32[]{:S(2)}, u32[]{:S(2)}) async-start(bf16[96,24,768]{0,1,2:T(8,128)(2,1)} %copy.99), calls=%async_computation.2 | async-start | bytes 9437184 | tf_op jit(solution)/shard_map/all_to_all | solution.py:140
  66.3 68.7 %all-to-all-done.2 = bf16[96,24,768]{0,1,2:T(8,128)(2,1)} async-done(((bf16[96,24,768]{0,1,2:T(8,128)(2,1)}), bf16[96,24,768]{0,1,2:T(8,128)(2,1)}, u32[]{:S(2)}, u32[]{:S(2)}) %all-to-all-start.2) | async-done | bytes 3538976 | tf_op jit(solution)/shard_map/all_to_all | solution.py:140
  135.0 5.6 copy.101
  140.6 7.4 %copy.102 = bf16[96,384,48]{1,2,0:T(8,128)(2,1)} copy(bf16[96,384,48]{0,2,1:T(8,128)(2,1)} %bitcast.239) | data formatting | bytes 7077888 | tf_op jit(solution)/shard_map/all_to_all | solution.py:140
  148.0 6.2 fusion.85
  154.3 4.1 fusion.91
  170.3 4.5 fusion.25
  174.8 4.9 fusion.27
  182.3 4.2 pad_maximum_fusion.1
  186.5 7.1 %copy.114 = bf16[96,384,2,24]{0,3,2,1:T(8,128)(2,1)} copy(bf16[96,384,2,24]{1,3,2,0:T(8,128)(2,1)} %pad_maximum_fusion.1) | data formatting | bytes 7077888 | tf_op jit(solution)/shard_map/stack | solution.py:86
  193.7 8.6 %all-to-all-start.3 = ((bf16[96,384,48]{0,2,1:T(8,128)(2,1)}), bf16[96,384,48]{0,2,1:T(8,128)(2,1)}, u32[]{:S(2)}, u32[]{:S(2)}) async-start(bf16[96,384,48]{0,2,1:T(8,128)(2,1)} %bitcast.238), calls=%async_computation.3 | async-start | bytes 9437184 | tf_op jit(solution)/shard_map/all_to_all | solution.py:154
  203.5 55.3 %all-to-all-done.3 = bf16[96,384,48]{0,2,1:T(8,128)(2,1)} async-done(((bf16[96,384,48]{0,2,1:T(8,128)(2,1)}), bf16[96,384,48]{0,2,1:T(8,128)(2,1)}, u32[]{:S(2)}, u32[]{:S(2)}) %all-to-all-start.3) | async-done | bytes 3538976 | tf_op jit(solution)/shard_map/all_to_all | solution.py:154
  258.8 5.8 copy.115
  264.6 6.7 %copy.116 = bf16[96,24,768]{2,1,0:T(8,128)(2,1)} copy(bf16[96,24,768]{0,2,1:T(8,128)(2,1)} %bitcast.240) | data formatting | bytes 7077888 | tf_op jit(solution)/shard_map/dot_general | solution.py:155
  271.3 20.3 %fusion = (f32[]{:T(128)}, f32[]{:T(128)}, f32[96,24,768]{2,1,0:T(8,128)}) fusion(f32[24]{0:T(128)} %add_cosine_fusion, bf16[96,24,768]{2,1,0:T(8,128)(2,1)S(1)} %copy-done, f32[96]{0:T(128)S(1)} %get-tuple-element.40, f32[96]{0:T(128)S(1)} %get-tuple-element.46, f32[24,768]{1,0:T(8,128)} %copy-done.5, f32[24,768]{1,0:T(8,128)} %copy-done.4, ...), kind=kOutput, calls=%fused_computation.10 | convolution fusion | flops 2754478080 | bytes 14311016 | tf_op jit(solution)/shard_map/dot_general | solution.py:155
  291.6 6.6 %all-reduce.2 = (f32[]{:T(128)}, f32[]{:T(128)}) all-reduce(f32[]{:T(128)} %get-tuple-element.6, f32[]{:T(128)} %get-tuple-element.5), channel_id=1, replica_groups=mesh['lat_0'=4,'lat_1'=4,'ch_0'=4,'ch_1'=2] {'lat_0'}, use_global_device_ids=true, to_apply=%region_5.6 | all-reduce | flops 2 | bytes 16 | tf_op jit(solution)/shard_map/psum | solution.py:30
  298.3 11.6 %all-reduce.1 = (f32[]{:T(128)}, f32[]{:T(128)}) all-reduce(f32[]{:T(128)} %get-tuple-element.11, f32[]{:T(128)} %get-tuple-element.12), channel_id=1, replica_groups=mesh['lat_0'=4,'lat_1'=4,'ch_0'=4,'ch_1'=2] {'lat_1'}, use_global_device_ids=true, to_apply=%region_6.7 | all-reduce | flops 2 | bytes 16 | tf_op jit(solution)/shard_map/psum | solution.py:30
  309.9 11.0 %all-reduce = (f32[]{:T(128)}, f32[]{:T(128)}) all-reduce(f32[]{:T(128)} %get-tuple-element.9, f32[]{:T(128)} %get-tuple-element.10), channel_id=1, replica_groups=mesh['lat_0'=4,'lat_1'=4,'ch_0'=4,'ch_1'=2] {'ch_0'}, use_global_device_ids=true, to_apply=%region_7.8 | all-reduce | flops 2 | bytes 16 | tf_op jit(solution)/shard_map/psum | solution.py:30
  320.9 11.2 %all-reduce.3 = (f32[]{:T(128)}, f32[]{:T(128)}) all-reduce(f32[]{:T(128)} %get-tuple-element.7, f32[]{:T(128)} %get-tuple-element.8), channel_id=1, replica_groups=mesh['lat_0'=4,'lat_1'=4,'ch_0'=4,'ch_1'=2] {'ch_1'}, use_global_device_ids=true, to_apply=%region_8.9 | all-reduce | flops 2 | bytes 16 | tf_op jit(solution)/shard_map/psum | solution.py:30
  333.5 4.9 fusion.190
  340.9 10.7 %all_to_all.86 = bf16[8,24,768]{2,1,0:T(8,128)(2,1)S(1)} all-to-all(bf16[8,24,768]{2,1,0:T(8,128)(2,1)S(1)} %broadcast_in_dim.52), channel_id=1, replica_groups=mesh['lat_0'=4,'lat_1'=4,'ch_0'=4,'ch_1'=2] {'ch_0','ch_1'}, dimensions={0} | all-to-all | bytes 589824 | tf_op jit(solution)/shard_map/all_to_all | solution.py:21
  352.3 3.9 all-to-all-start.4
  356.2 6.8 %all-to-all-done.4 = bf16[8,24,768]{2,1,0:T(8,128)(2,1)S(1)} async-done(((bf16[8,24,768]{2,1,0:T(8,128)(2,1)}), bf16[8,24,768]{2,1,0:T(8,128)(2,1)S(1)}, u32[]{:S(2)}, u32[]{:S(2)}) %all-to-all-start.4) | async-done | bytes 294944 | tf_op jit(solution)/shard_map/all_to_all | solution.py:21
  363.1 3.4 fusion.4
  366.5 15.1 %convolution_convert_fusion = bf16[2304,768]{1,0:T(8,128)(2,1)S(1)} fusion(bf16[2304,768]{1,0:T(8,128)(2,1)S(1)} %bitcast.247, s32[768]{0:T(1024)S(1)} %copy-done.13, pred[768]{0:T(1024)(128)(4,1)S(1)} %copy-done.22), kind=kOutput, calls=%fused_computation.25 | convolution fusion | flops 2727936000 | bytes 7081728 | tf_op jit(solution)/shard_map/dot_general | solution.py:135
  381.6 5.1 copy.117
  386.7 58.5 %all_to_all.87 = bf16[96,24,768]{0,1,2:T(8,128)(2,1)S(1)} all-to-all(bf16[96,24,768]{0,1,2:T(8,128)(2,1)} %copy.117), channel_id=1, replica_groups=mesh['lat_0'=4,'lat_1'=4,'ch_0'=4,'ch_1'=2] {'lat_0','lat_1'}, dimensions={2} | all-to-all | bytes 7077888 | tf_op jit(solution)/shard_map/all_to_all | solution.py:140
  448.3 6.4 %copy.120 = bf16[96,384,48]{1,2,0:T(8,128)(2,1)S(1)} copy(bf16[96,384,48]{0,2,1:T(8,128)(2,1)} %bitcast.241) | data formatting | bytes 7077888 | tf_op jit(solution)/shard_map/all_to_all | solution.py:140
  454.7 4.1 fusion.82
  458.8 4.1 fusion.88
  474.8 4.4 fusion.21
  479.3 4.8 fusion.23
  489.2 5.3 copy.132
  494.5 58.4 %all_to_all.88 = bf16[96,384,48]{0,2,1:T(8,128)(2,1)S(1)} all-to-all(bf16[96,384,48]{0,2,1:T(8,128)(2,1)} %bitcast.242), channel_id=1, replica_groups=mesh['lat_0'=4,'lat_1'=4,'ch_0'=4,'ch_1'=2] {'lat_0','lat_1'}, dimensions={1} | all-to-all | bytes 7077888 | tf_op jit(solution)/shard_map/all_to_all | solution.py:154
  552.8 3.4 copy.133
  556.2 7.0 %copy.134 = bf16[96,24,768]{2,1,0:T(8,128)(2,1)} copy(bf16[96,24,768]{0,2,1:T(8,128)(2,1)} %bitcast.243) | data formatting | bytes 7077888 | tf_op jit(solution)/shard_map/dot_general | solution.py:155
  563.3 19.7 %fusion.6 = (f32[]{:T(128)}, f32[96,24,768]{2,1,0:T(8,128)}) fusion(f32[24]{0:T(128)} %add_cosine_fusion, bf16[96,24,768]{2,1,0:T(8,128)(2,1)S(1)} %copy-done.2, f32[96]{0:T(128)S(1)} %get-tuple-element.39, f32[96]{0:T(128)S(1)} %get-tuple-element.47, f32[24,768]{1,0:T(8,128)} %copy-done.7, f32[24,768]{1,0:T(8,128)} %copy-done.6, ...), kind=kOutput, calls=%fused_computation.16 | convolution fusion | flops 2749169664 | bytes 14311012 | tf_op jit(solution)/shard_map/dot_general | solution.py:155
  582.9 8.4 %psum.92 = f32[]{:T(128)} all-reduce(f32[]{:T(128)} %get-tuple-element.44), channel_id=1, replica_groups=mesh['lat_0'=4,'lat_1'=4,'ch_0'=4,'ch_1'=2] {'lat_0'}, use_global_device_ids=true, to_apply=%region_19.20 | all-reduce | flops 1 | bytes 8 | tf_op jit(solution)/shard_map/psum | solution.py:30
  591.4 6.9 %psum.93 = f32[]{:T(128)} all-reduce(f32[]{:T(128)} %psum.92), channel_id=1, replica_groups=mesh['lat_0'=4,'lat_1'=4,'ch_0'=4,'ch_1'=2] {'lat_1'}, use_global_device_ids=true, to_apply=%region_20.21 | all-reduce | flops 1 | bytes 8 | tf_op jit(solution)/shard_map/psum | solution.py:30
  598.2 7.5 %psum.94 = f32[]{:T(128)} all-reduce(f32[]{:T(128)} %psum.93), channel_id=1, replica_groups=mesh['lat_0'=4,'lat_1'=4,'ch_0'=4,'ch_1'=2] {'ch_0'}, use_global_device_ids=true, to_apply=%region_21.22 | all-reduce | flops 1 | bytes 8 | tf_op jit(solution)/shard_map/psum | solution.py:30
  605.7 12.1 %psum.95 = f32[]{:T(128)} all-reduce(f32[]{:T(128)} %psum.94), channel_id=1, replica_groups=mesh['lat_0'=4,'lat_1'=4,'ch_0'=4,'ch_1'=2] {'ch_1'}, use_global_device_ids=true, to_apply=%region_22.23 | all-reduce | flops 1 | bytes 8 | tf_op jit(solution)/shard_map/psum | solution.py:30
  619.2 5.7 multiply_convert_fusion
  (97 shorter events, 54.0 us)
Async XLA Ops:
  0.0 10.6 %copy-start = (bf16[96,24,768]{2,1,0:T(8,128)(2,1)S(1)}, bf16[96,24,768]{2,1,0:T(8,128)(2,1)}, u32[]{:S(2)}) copy-start(bf16[96,24,768]{2,1,0:T(8,128)(2,1)} %param.6) | copy-start | bytes 10616836
  4.8 12.7 %all-to-all-start = ((bf16[8,24,768]{2,1,0:T(8,128)(2,1)}), bf16[8,24,768]{2,1,0:T(8,128)(2,1)}, u32[]{:S(2)}, u32[]{:S(2)}) async-start(bf16[8,24,768]{2,1,0:T(8,128)(2,1)} %broadcast_in_dim.45), calls=%async_computation | async-start | bytes 589824 | tf_op jit(solution)/shard_map/all_to_all | solution.py:21
  10.6 1.4 copy-start.19
  10.6 1.4 copy-start.20
  19.0 11.9 %all-to-all-start.1 = ((bf16[8,24,768]{2,1,0:T(8,128)(2,1)}), bf16[8,24,768]{2,1,0:T(8,128)(2,1)}, u32[]{:S(2)}, u32[]{:S(2)}) async-start(bf16[8,24,768]{2,1,0:T(8,128)(2,1)} %broadcast_in_dim.46), calls=%async_computation.1 | async-start | bytes 589824 | tf_op jit(solution)/shard_map/all_to_all | solution.py:21
  32.8 1.4 copy-start.4
  32.8 1.4 copy-start.5
  32.8 1.4 copy-start.12
  32.9 1.4 copy-start.21
  57.3 77.8 %all-to-all-start.2 = ((bf16[96,24,768]{0,1,2:T(8,128)(2,1)}), bf16[96,24,768]{0,1,2:T(8,128)(2,1)}, u32[]{:S(2)}, u32[]{:S(2)}) async-start(bf16[96,24,768]{0,1,2:T(8,128)(2,1)} %copy.99), calls=%async_computation.2 | async-start | bytes 9437184 | tf_op jit(solution)/shard_map/all_to_all | solution.py:140
  148.0 6.3 %copy-start.3 = (bf16[96,384,48]{1,2,0:T(8,128)(2,1)S(1)}, bf16[96,384,48]{1,2,0:T(8,128)(2,1)}, u32[]{:S(2)}) copy-start(bf16[96,384,48]{1,2,0:T(8,128)(2,1)} %copy.102) | copy-start | bytes 10616836
  160.6 1.2 copy-start.8
  162.7 0.7 copy-start.18
  163.4 0.7 copy-start.17
  164.0 0.9 copy-start.10
  193.7 65.1 %all-to-all-start.3 = ((bf16[96,384,48]{0,2,1:T(8,128)(2,1)}), bf16[96,384,48]{0,2,1:T(8,128)(2,1)}, u32[]{:S(2)}, u32[]{:S(2)}) async-start(bf16[96,384,48]{0,2,1:T(8,128)(2,1)} %bitcast.238), calls=%async_computation.3 | async-start | bytes 9437184 | tf_op jit(solution)/shard_map/all_to_all | solution.py:154
  338.3 1.8 copy-start.1
  352.3 10.7 %all-to-all-start.4 = ((bf16[8,24,768]{2,1,0:T(8,128)(2,1)}), bf16[8,24,768]{2,1,0:T(8,128)(2,1)S(1)}, u32[]{:S(2)}, u32[]{:S(2)}) async-start(bf16[8,24,768]{2,1,0:T(8,128)(2,1)} %broadcast_in_dim.51), calls=%async_computation.4 | async-start | bytes 589824 | tf_op jit(solution)/shard_map/all_to_all | solution.py:21
  363.1 3.4 copy-start.6
  363.1 3.4 copy-start.7
  363.1 3.4 copy-start.13
  363.1 3.4 copy-start.22
  463.9 1.2 copy-start.9
  467.2 0.7 copy-start.16
  467.8 0.9 copy-start.11
  468.7 0.7 copy-start.15
  556.2 7.0 %copy-start.2 = (bf16[96,24,768]{2,1,0:T(8,128)(2,1)S(1)}, bf16[96,24,768]{2,1,0:T(8,128)(2,1)}, u32[]{:S(2)}) copy-start(bf16[96,24,768]{2,1,0:T(8,128)(2,1)} %copy-done.1) | copy-start | bytes 10616836
  556.2 7.0 %copy-start.14 = (f32[768]{0:T(1024)S(1)}, f32[768]{0:T(1024)}, u32[]{:S(2)}) copy-start(f32[768]{0:T(1024)} %compare_select_fusion) | copy-start | bytes 9220
where the time goes:
time: 633 us; the launch traced here: 625 us
  blocking collectives  203 us (32%)
  waiting for transfers between devices  140 us (22%)
  matrix products  124 us (20%)
  local copies, waits for them, and re-layouts  78.5 us (12%)
  other arithmetic  45.1 us (7%)
  starting transfers between devices  31.1 us (5%)
    psum x8, blocking collectives, by_axis(): return functools.reduce(lax.psum, axes, x)  75.4 us
    all_to_all x1, waiting for transfers between devices, per_device(): lax.all_to_all(lon_spec.reshape(ch_dev, band_rows, lon_cells), LAT, split...  68.7 us
    all_to_all x1, blocking collectives, per_device(): lax.all_to_all(lon_spec.reshape(ch_dev, band_rows, lon_cells), LAT, split...  58.5 us
    all_to_all x1, blocking collectives, per_device(): lax.all_to_all(back_spec, LAT, split_axis=1, concat_axis=2, tiled=True)  58.4 us
    all_to_all x1, waiting for transfers between devices, per_device(): lax.all_to_all(back_spec, LAT, split_axis=1, concat_axis=2, tiled=True)  55.3 us
    dot_general x2, matrix products, per_device(): jnp.dot(band_spec.reshape(ch_dev * band_rows, lon_cells), inverse, prefer...  40 us
    dot_general x2, matrix products, per_device(): jnp.dot(normed.reshape(ch_dev * band_rows, lon_cells), forward, preferred...  31 us
    all_to_all x4, local copies, waits for them, and re-layouts, per_device(): lax.all_to_all(lon_spec.reshape(ch_dev, band_rows, lon_cells), LAT, split...  22.5 us
  transfers between devices with their start and end apart: 5, of which 5 were waited for; matrix products, arithmetic and copies ran while one was open for 1% of the time, Pallas kernels for 0%

commit v1 on v0

v1 whole, which is shorter than its diff:
```python
import math

import jax
import jax.numpy as jnp
from jax import lax
from jax.experimental import pallas as pl
from jax.experimental.pallas import tpu as pltpu
from jax.sharding import Mesh
from jax.sharding import PartitionSpec as P

CH = ("ch_0", "ch_1")
LAT = ("lat_0", "lat_1")
MESH = pl.DeviceIdType.MESH

norm_eps = 1e-05
shrink_level = 0.01

F32 = jnp.float32
BF16 = jnp.bfloat16

N_LAT = 16
BAND = 24
CHN = 96
ROWS = CHN * BAND
LON = 768
LATS = N_LAT * BAND
CHUNKS = 3
KL = 8
ALL_CH = 768
PIECE = 12 * BAND

ORDER = [
    (1, 1), (3, 3), (2, 2), (1, 0), (3, 0), (0, 1), (0, 3), (1, 3), (3, 1),
    (2, 0), (0, 2), (1, 2), (3, 2), (2, 1), (2, 3),
]
CH_ORDER = [(1, 0), (3, 0), (1, 1), (3, 1), (2, 0), (2, 1), (0, 1)]


def trig(length, n, f):
    phase = n * f % length
    ang = phase.astype(F32) * (2.0 * math.pi / length)
    scale = 1.0 / math.sqrt(length)
    return jnp.cos(ang) * scale, jnp.sin(ang) * scale


def lon_table():
    row = jnp.arange(LON, dtype=jnp.int32)
    c = row // 256
    half = row // 128 % 2
    kk = row // 8 % 16
    q = half * 8 + row % 8
    mode = q * BAND + c * KL + kk % KL
    w = jnp.arange(LON, dtype=jnp.int32)
    cs, sn = trig(LON, mode[:, None], w[None, :])
    return jnp.where((kk < KL)[:, None], cs, -sn).astype(BF16).reshape(CHUNKS, 256, LON)


def lat_tables():
    n = jnp.arange(LATS, dtype=jnp.int32)
    cs, sn = trig(LATS, n[:, None], n[None, :])
    return cs.astype(BF16), sn.astype(BF16)


def kernel(
    x_ref, tb_ref, cl_ref, sl_ref, a1_ref, b1_ref, a2_ref, area_ref, gain_ref, shift_ref,
    o_ref,
    V, N, TF, TI, LF, LI, SF, RF, SB, RB, G, R, SP, MX,
    ST, RS, RED, AG, ES, EB, TG, MI,
    fs, fr, bs, br, rss, rsr, ags, agr, es, er,
):
    y = lax.axis_index("lat_0")
    z = lax.axis_index("lat_1")
    cx = lax.axis_index("ch_0")
    ck = lax.axis_index("ch_1")
    me = y * 4 + z
    mc = cx * 2 + ck

    def lat_to(a, b):
        yy = lax.rem(y + a, 4)
        zz = lax.rem(z + b, 4)
        return {"lat_0": yy, "lat_1": zz}, yy * 4 + zz

    def ch_to(a, b):
        xx = lax.rem(cx + a, 4)
        kk = lax.rem(ck + b, 2)
        return {"ch_0": xx, "ch_1": kk}, xx * 2 + kk

    bar = pltpu.get_barrier_semaphore()
    for a, b in ORDER:
        pl.semaphore_signal(bar, 1, device_id=lat_to(a, b)[0], device_id_type=MESH)
    for a, b in CH_ORDER:
        pl.semaphore_signal(bar, 1, device_id=ch_to(a, b)[0], device_id_type=MESH)
    pl.semaphore_wait(bar, len(ORDER) + len(CH_ORDER))

    def rcopy(src, dst, ss, rr, dev):
        return pltpu.make_async_remote_copy(
            src_ref=src, dst_ref=dst, send_sem=ss, recv_sem=rr, device_id=dev, device_id_type=MESH
        )

    def exchange_start(sb, rb, ss, rr, c):
        for a, b in ORDER:
            dev, q = lat_to(a, b)
            rcopy(sb.at[c, q], rb.at[c, me], ss.at[c, q], rr.at[c, me], dev).start()
        rb[c, me] = sb[c, me]

    def exchange_recv(sb, rb, ss, rr, c):
        for a, b in ORDER:
            dev, p = lat_to(4 - a, 4 - b)
            rcopy(sb.at[c, p], rb.at[c, p], ss.at[c, p], rr.at[c, p], dev).wait_recv()

    def exchange_sent(sb, rb, ss, rr, c):
        for a, b in ORDER:
            dev, q = lat_to(a, b)
            rcopy(sb.at[c, q], rb.at[c, me], ss.at[c, q], rr.at[c, me], dev).wait_send()

    def partial_sums(load):
        def step(i, carry):
            s1, s2 = carry
            for v in load(i):
                s1 = s1 + v
                s2 = s2 + v * v
            return s1, s2

        zero = jnp.zeros((BAND, LON), F32)
        s1, s2 = lax.fori_loop(0, CHN // 2, step, (zero, zero))
        for hb in range(3):
            for lb in range(6):
                ST[hb * 6 + lb] = s1[8 * hb : 8 * hb + 8, 128 * lb : 128 * lb + 128]
                ST[18 + hb * 6 + lb] = s2[8 * hb : 8 * hb + 8, 128 * lb : 128 * lb + 128]
        for t in range(36, 40):
            ST[t] = jnp.zeros((8, 128), F32)
        e = jnp.zeros((8, 128), F32)
        for hb in range(3):
            for lb in range(6):
                e = e + ST[18 + hb * 6 + lb] * area_ref[8 * hb : 8 * hb + 8, :]
        ES[...] = e

    def load_input(i):
        xx = x_ref[pl.ds(pl.multiple_of(i * 48, 48), 48), :].astype(F32)
        V[pl.ds(pl.multiple_of(i * 48, 48), 48), :] = xx
        return xx[0:24], xx[24:48]

    def load_v(i):
        return (
            V[pl.ds(pl.multiple_of(i * 48, 48), 24), :],
            V[pl.ds(pl.multiple_of(i * 48 + 24, 24), 24), :],
        )

    def e_copy(a, b):
        dev, q = lat_to(a, b)
        return rcopy(ES, EB.at[me], es.at[q], er.at[me], dev)

    def e_from(a, b):
        dev, p = lat_to(4 - a, 4 - b)
        return rcopy(ES, EB.at[p], es.at[p], er.at[p], dev)

    def rs_copy(a, b):
        dev, d = ch_to(a, b)
        return rcopy(ST.at[pl.ds(5 * d, 5)], RS.at[mc], rss.at[d], rsr.at[mc], dev)

    def rs_from(a, b):
        dev, d = ch_to(4 - a, 2 - b)
        return rcopy(ST.at[pl.ds(5 * d, 5)], RS.at[d], rss.at[d], rsr.at[d], dev)

    def ag_copy(a, b):
        dev, d = ch_to(a, b)
        return rcopy(RED, AG.at[mc], ags.at[d], agr.at[mc], dev)

    def ag_from(a, b):
        dev, d = ch_to(4 - a, 2 - b)
        return rcopy(RED, AG.at[d], ags.at[d], agr.at[d], dev)

    def exchange_stats(between):
        for a, b in CH_ORDER:
            rs_copy(a, b).start()
        for a, b in ORDER:
            e_copy(a, b).start()
        RS[mc] = ST[pl.ds(5 * mc, 5)]
        EB[me] = ES[...]
        between()
        for a, b in CH_ORDER:
            rs_from(a, b).wait_recv()
        tot = RS[0]
        for d in range(1, 8):
            tot = tot + RS[d]
        RED[0:5] = tot
        for a, b in ORDER:
            e_from(a, b).wait_recv()
        e = EB[0]
        for p in range(1, N_LAT):
            e = e + EB[p]
        RED[5] = e
        for a, b in CH_ORDER:
            ag_copy(a, b).start()
        AG[mc] = RED[...]
        for a, b in CH_ORDER:
            ag_from(a, b).wait_recv()
        for a, b in CH_ORDER:
            rs_copy(a, b).wait_send()
            ag_copy(a, b).wait_send()
        for a, b in ORDER:
            e_copy(a, b).wait_send()
        e = AG[0, 5]
        for d in range(1, 8):
            e = e + AG[d, 5]
        e = jnp.sum(e, axis=0, keepdims=True)
        e = jnp.sum(e, axis=1, keepdims=True)
        return jnp.broadcast_to(e, (8, 128))

    def lane_masks():
        lane = lax.broadcasted_iota(jnp.int32, (48, 128), 1) & 7
        return [lane == s for s in range(8)]

    def block_swap(parts, masks):
        rolled = [p if r == 0 else pltpu.roll(p, r, 1) for r, p in enumerate(parts)]
        out = []
        for q in range(8):
            acc = rolled[-q % 8]
            for s in range(1, 8):
                acc = jnp.where(masks[s], rolled[(s - q) % 8], acc)
            out.append(acc if q == 0 else pltpu.roll(acc, 128 - q, 1))
        return out

    def forward_chunk(c, _):
        def step(i, _):
            base = pl.multiple_of(i * 384, 384)
            R[...] = jnp.dot(N[pl.ds(base, 384), :], TF[c], preferred_element_type=F32)
            masks = lane_masks()
            for half in range(2):
                hs = slice(128 * half, 128 * half + 128)
                parts = [
                    jnp.concatenate(
                        [R[24 * r : 24 * r + 24, hs], R[192 + 24 * r : 216 + 24 * r, hs]], axis=0
                    )
                    for r in range(8)
                ]
                for q, piece in enumerate(block_swap(parts, masks)):
                    SF[c, 8 * half + q, pl.ds(pl.multiple_of(i * 48, 48), 48), :] = piece.astype(BF16)
            return 0

        lax.fori_loop(0, 6, step, 0)
        exchange_start(SF, RF, fs, fr, c)
        return 0

    def middle_chunk(l, c):
        exchange_recv(SF, RF, fs, fr, c)

        def gather(i, _):
            rows = pl.ds(pl.multiple_of(i * 48, 48), 48)
            got = [RF[c, p, rows, :].astype(F32) for p in range(N_LAT)]
            for j in range(2):
                blk = jnp.concatenate([g[24 * j : 24 * j + 24] for g in got], axis=0)
                t = blk.T.reshape(16, 8, LATS)
                G[:, pl.ds(pl.multiple_of(i * 16 + 8 * j, 8), 8), :] = t
            return 0

        lax.fori_loop(0, 6, gather, 0)

        def mix(b, _):
            g_re = G[pl.ds(4 * b, 4)].reshape(384, LATS).astype(BF16)
            g_im = G[pl.ds(8 + 4 * b, 4)].reshape(384, LATS).astype(BF16)
            SP[...] = jnp.dot(
                jnp.concatenate([g_re, g_im], axis=1), LF[...], preferred_element_type=F32
            ).astype(BF16)

            for k in range(4):
                rows = slice(96 * k, 96 * k + 96)
                both = jnp.concatenate([SP[rows, 0:LATS], SP[rows, LATS:]], axis=0)
                hid = jnp.dot(a1_ref[l], both, preferred_element_type=F32) + b1_ref[l]
                hid = jnp.maximum(hid, 0.0).astype(BF16)
                m = jnp.dot(a2_ref[l], hid, preferred_element_type=F32)
                m = (m - jnp.clip(m, -shrink_level, shrink_level)).astype(BF16)
                MX[rows, 0:LATS] = m[0:96]
                MX[rows, LATS:] = m[96:192]
            back = jnp.dot(MX[...], LI[...], preferred_element_type=F32)
            G[pl.ds(4 * b, 4)] = back[:, 0:LATS].reshape(4, CHN, LATS)
            G[pl.ds(8 + 4 * b, 4)] = back[:, LATS:].reshape(4, CHN, LATS)
            return 0

        lax.fori_loop(0, 2, mix, 0)

        def scatter(i, _):
            ts = []
            for j in range(2):
                blk = G[:, pl.ds(pl.multiple_of(i * 16 + 8 * j, 8), 8), :].reshape(128, LATS)
                ts.append(blk.T)
            for p in range(N_LAT):
                piece = jnp.concatenate([t[24 * p : 24 * p + 24] for t in ts], axis=0)
                SB[c, p, pl.ds(pl.multiple_of(i * 48, 48), 48), :] = piece.astype(BF16)
            return 0

        lax.fori_loop(0, 6, scatter, 0)
        exchange_start(SB, RB, bs, br, c)

    def backward_chunk(c, _):
        exchange_recv(SB, RB, bs, br, c)

        def step(i, _):
            rows = pl.ds(pl.multiple_of(i * 48, 48), 48)
            masks = lane_masks()
            for half in range(2):
                hs = slice(128 * half, 128 * half + 128)
                parts = [RB[c, 8 * half + q, rows, :].astype(F32) for q in range(8)]
                for r, piece in enumerate(block_swap(parts, masks)):
                    R[24 * r : 24 * r + 24, hs] = piece[0:24]
                    R[192 + 24 * r : 216 + 24 * r, hs] = piece[24:48]
            base = pl.multiple_of(i * 384, 384)
            V[pl.ds(base, 384), :] += jnp.dot(
                R[...].astype(BF16), TI[c], preferred_element_type=F32
            )
            return 0

        lax.fori_loop(0, 6, step, 0)
        return 0

    def set_tables():
        row = lax.broadcasted_iota(jnp.int32, (256, LON), 0)
        for c in range(CHUNKS):
            t = tb_ref[c].astype(F32)
            TF[c] = t.T.astype(BF16)
            twice = t * 2.0
            TI[c] = (jnp.where(row == 0, t, twice) if c == 0 else twice).astype(BF16)
        cl = cl_ref[...]
        sl = sl_ref[...]
        LF[0:LATS, 0:LATS] = cl
        LF[0:LATS, LATS:] = -sl
        LF[LATS:, 0:LATS] = sl
        LF[LATS:, LATS:] = cl
        LI[0:LATS, 0:LATS] = cl
        LI[0:LATS, LATS:] = sl
        LI[LATS:, 0:LATS] = -sl
        LI[LATS:, LATS:] = cl

    def normalize(l, scale):
        for hb in range(3):
            for lb in range(6):
                t = hb * 6 + lb
                mean = AG[t // 5, t % 5] * scale * (1.0 / ALL_CH)
                u = t + 18
                spread = AG[u // 5, u % 5] * (scale * scale) * (1.0 / ALL_CH) - mean * mean
                MI[0, 8 * hb : 8 * hb + 8, 128 * lb : 128 * lb + 128] = mean
                MI[1, 8 * hb : 8 * hb + 8, 128 * lb : 128 * lb + 128] = lax.rsqrt(spread + norm_eps)
        srow = scale[0:1, 0:1]

        def step(i, _):
            base = pl.multiple_of(i * 48, 48)
            for lb in range(2):
                ls = slice(384 * lb, 384 * lb + 384)
                mean = MI[0, :, ls]
                inv = MI[1, :, ls]
                both = []
                for j in range(2):
                    rows = pl.ds(pl.multiple_of(i * 48 + 24 * j, 24), 24)
                    cur = (V[rows, ls] * srow).astype(BF16).astype(F32)
                    nrm = (cur - mean) * inv * gain_ref[l, 2 * i + j] + shift_ref[l, 2 * i + j]
                    nrm = nrm.astype(BF16)
                    V[rows, ls] = cur + nrm.astype(F32)
                    both.append(nrm.astype(F32))
                N[pl.ds(base, 48), ls] = jnp.concatenate(both, axis=0).astype(BF16)
            return 0

        lax.fori_loop(0, CHN // 2, step, 0)

    def layer(l, scale):
        normalize(l, scale)
        lax.fori_loop(0, CHUNKS, forward_chunk, 0)

        def mid(c, _):
            middle_chunk(l, c)
            return 0

        lax.fori_loop(0, CHUNKS, mid, 0)
        lax.fori_loop(0, CHUNKS, backward_chunk, 0)

        def sent(c, _):
            exchange_sent(SF, RF, fs, fr, c)
            exchange_sent(SB, RB, bs, br, c)
            return 0

        lax.fori_loop(0, CHUNKS, sent, 0)
        partial_sums(load_v)
        energy = exchange_stats(lambda: None)
        return jnp.sqrt(TG[...] / energy)

    partial_sums(load_input)
    TG[...] = exchange_stats(set_tables)
    scale = lax.fori_loop(0, 2, layer, jnp.ones((8, 128), F32))

    srow = scale[0:1, 0:1]

    def finish(i, _):
        rows = pl.ds(pl.multiple_of(i * 48, 48), 48)
        o_ref[rows, :] = (V[rows, :] * srow).astype(BF16)
        return 0

    lax.fori_loop(0, CHN // 2, finish, 0)


def complex_block(w):
    re = jnp.swapaxes(w[:, 0], 1, 2)
    im = jnp.swapaxes(w[:, 1], 1, 2)
    top = jnp.concatenate([re, -im], axis=2)
    low = jnp.concatenate([im, re], axis=2)
    return jnp.concatenate([top, low], axis=1)


def per_device(field_in, ln_gain, ln_shift, mix_first, mix_bias, mix_second):
    layers = mix_first.shape[0]
    a1 = complex_block(mix_first[:, :, 0])
    a2 = complex_block(mix_second[:, :, 0])
    b1 = mix_bias[:, :, 0].astype(F32).reshape(layers, 2 * CHN, 1)
    cl, sl = lat_tables()
    row = (lax.axis_index(LAT) * BAND + jnp.arange(BAND, dtype=jnp.int32)).astype(F32)
    area = jnp.cos((row + 0.5) * (math.pi / LATS) - 0.5 * math.pi)
    area = jnp.broadcast_to(area[:, None], (BAND, 128))
    vm = pl.BlockSpec(memory_space=pltpu.VMEM)
    sm = pl.BlockSpec(memory_space=pltpu.SMEM)
    dma = pltpu.SemaphoreType.DMA
    out = pl.pallas_call(
        kernel,
        out_shape=jax.ShapeDtypeStruct((ROWS, LON), BF16),
        in_specs=[vm] * 8 + [sm] * 2,
        out_specs=vm,
        scratch_shapes=[
            pltpu.VMEM((ROWS, LON), F32),
            pltpu.VMEM((ROWS, LON), BF16),
            pltpu.VMEM((CHUNKS, LON, 256), BF16),
            pltpu.VMEM((CHUNKS, 256, LON), BF16),
            pltpu.VMEM((2 * LATS, 2 * LATS), BF16),
            pltpu.VMEM((2 * LATS, 2 * LATS), BF16),
            pltpu.VMEM((CHUNKS, N_LAT, PIECE, 128), BF16),
            pltpu.VMEM((CHUNKS, N_LAT, PIECE, 128), BF16),
            pltpu.VMEM((CHUNKS, N_LAT, PIECE, 128), BF16),
            pltpu.VMEM((CHUNKS, N_LAT, PIECE, 128), BF16),
            pltpu.VMEM((16, CHN, LATS), F32),
            pltpu.VMEM((384, 256), F32),
            pltpu.VMEM((384, 2 * LATS), BF16),
            pltpu.VMEM((384, 2 * LATS), BF16),
            pltpu.VMEM((40, 8, 128), F32),
            pltpu.VMEM((8, 5, 8, 128), F32),
            pltpu.VMEM((6, 8, 128), F32),
            pltpu.VMEM((8, 6, 8, 128), F32),
            pltpu.VMEM((8, 128), F32),
            pltpu.VMEM((N_LAT, 8, 128), F32),
            pltpu.VMEM((8, 128), F32),
            pltpu.VMEM((2, BAND, LON), F32),
            dma((CHUNKS, N_LAT)),
            dma((CHUNKS, N_LAT)),
            dma((CHUNKS, N_LAT)),
            dma((CHUNKS, N_LAT)),
            dma((8,)),
            dma((8,)),
            dma((8,)),
            dma((8,)),
            dma((N_LAT,)),
            dma((N_LAT,)),
        ],
        compiler_params=pltpu.CompilerParams(
            collective_id=0, has_side_effects=True, vmem_limit_bytes=60 * 1024 * 1024
        ),
    )(
        field_in.reshape(ROWS, LON), lon_table(), cl, sl, a1, b1, a2, area, ln_gain, ln_shift
    )
    return out.reshape(CHN, BAND, LON)


def solution(mesh):
    finer = Mesh(mesh.devices.reshape(4, 4, 4, 2), ("lat_0", "lat_1", "ch_0", "ch_1"))
    in_specs = (
        P(CH, LAT, None),
        P(None, CH),
        P(None, CH),
        P(None, None, CH, None, None),
        P(None, None, CH, None),
        P(None, None, CH, None, None),
    )
    return jax.shard_map(
        per_device, mesh=finer, in_specs=in_specs, out_specs=P(CH, LAT, None), check_vma=False
    )
```

time: 633 us -> 255 us (0.40); the launches traced: 625 us -> 255 us
  Pallas kernels: 0 us -> 230 us
  blocking collectives: 203 us -> 0 us
  waiting for transfers between devices: 140 us -> 0 us
  matrix products: 124 us -> 0 us
  local copies, waits for them, and re-layouts: 78.5 us -> 8.24 us
  starting transfers between devices: 31.1 us -> 0 us
  other arithmetic: 45.1 us -> 15.9 us
    pallas_call x0 -> x1, Pallas kernels: none -> 230 us  [per_device(): pl.pallas_call(kernel, out_shape=jax.ShapeDtypeStruct((ROWS, LON), BF16),...]
    all_to_all x5 -> x0, waiting for transfers between devices: 140 us -> none  [the longest x1 68.7 us: per_device(): lax.all_to_all(lon_spec.reshape(ch_dev, band_rows, lon_cells), LAT, split...]
    all_to_all x3 -> x0, blocking collectives: 128 us -> none  [the longest x1 58.5 us: per_device(): lax.all_to_all(lon_spec.reshape(ch_dev, band_rows, lon_cells), LAT, split...]
    dot_general x28 -> x0, matrix products: 124 us -> none  [the longest x2 40 us: per_device(): jnp.dot(band_spec.reshape(ch_dev * band_rows, lon_cells), inverse, prefer...]
    psum x8 -> x0, blocking collectives: 75.4 us -> none  [by_axis(): return functools.reduce(lax.psum, axes, x)]
    all_to_all x6 -> x0, local copies, waits for them, and re-layouts: 31.7 us -> none  [the longest x4 22.5 us: per_device(): lax.all_to_all(lon_spec.reshape(ch_dev, band_rows, lon_cells), LAT, split...]
    all_to_all x5 -> x0, starting transfers between devices: 31.1 us -> none  [the longest x3 14.7 us: copy_for_each(): return lax.all_to_all(copies, axis, split_axis=0, concat_axis=0, tiled=True)]
    another operation x10 -> x0, other arithmetic: 17.8 us -> none
  transfers between devices with their start and end apart: 5 -> 0, of which waited for: 5 -> 0; matrix products, arithmetic and copies ran while one was open for 1% -> 0% of each run, Pallas kernels for 0% -> 0%
where the time goes in v1:
time: 255 us
  Pallas kernels  230 us (90%)
  other arithmetic  15.9 us (6%)
  local copies, waits for them, and re-layouts  8.24 us (3%)
    pallas_call x1, Pallas kernels, per_device(): pl.pallas_call(kernel, out_shape=jax.ShapeDtypeStruct((ROWS, LON), BF16),...  230 us
    convert_element_type x1, other arithmetic, lon_table(): jnp.where((kk < KL)[:, None], cs, -sn).astype(BF16)  11.6 us
    unnamed x3, local copies, waits for them, and re-layouts  6.01 us

profile of v1, /device:TPU:1, one launch (start us, length us, event | category | flops | bytes accessed | tf_op | source)
XLA Modules:
  0.0 254.7 jit_solution(15048313153115178591)
XLA Ops:
  0.1 0.7 broadcast_in_dim.8.area_ref
  0.8 1.0 copy.9
  1.8 1.0 copy.10
  2.8 0.9 maximum_maximum_fusion
  3.8 1.5 reshape.132.b1_ref
  5.3 3.3 %multiply_convert_fusion = (bf16[384,384]{1,0:T(8,128)(2,1)}, bf16[384,384]{1,0:T(8,128)(2,1)}) fusion(), kind=kLoop, calls=%fused_computation.11 | loop fusion | flops 1916928 | bytes 589824 | tf_op jit(solution)/shard_map/convert_element_type | solution.py:61
  8.6 11.6 %select_convert_fusion.tb_ref = bf16[3,256,768]{2,1,0:T(8,128)(2,1)} fusion(s32[3,256]{1,0:T(4,128)S(1)} %fusion.16, pred[3,256]{1,0:T(4,128)(4,1)S(1)} %broadcast_compare_fusion), kind=kLoop, calls=%fused_computation.3 | loop fusion | flops 8257536 | bytes 1183488 | tf_op jit(solution)/shard_map/convert_element_type | solution.py:55
  20.2 230.4 %shard_map.64 = bf16[2304,768]{1,0:T(8,128)(2,1)} custom-call(bf16[2304,768]{1,0:T(8,128)(2,1)} %bitcast.27, bf16[3,256,768]{2,1,0:T(8,128)(2,1)} %select_convert_fusion.tb_ref, bf16[384,384]{1,0:T(8,128)(2,1)} %get-tuple-element.10.cl_ref, bf16[384,384]{1,0:T(8,128)(2,1)} %get-tuple-element.9.sl_ref, bf16[2,192,192]{2,1,0:T(8,128)(2,1)} %get-tuple-element.11.a1_ref, ...), custom_call_target="tpu_custom_call" | custom-call | tf_op jit(solution)/shard_map/pallas_call | solution.py:419
  250.6 4.0 %copy.13 = bf16[96,24,768]{2,1,0:T(8,128)(2,1)} copy(bf16[96,24,768]{2,1,0:T(8,128)(2,1)} %bitcast.26) | data formatting | bytes 7077888
  (7 shorter events, 0.1 us)

commit v2 on v1

v2 whole, which is shorter than its diff:
```python
import math

import jax
import jax.numpy as jnp
import numpy as np
from jax import lax
from jax.experimental import pallas as pl
from jax.experimental.pallas import tpu as pltpu
from jax.sharding import Mesh
from jax.sharding import PartitionSpec as P

CH = ("ch_0", "ch_1")
LAT = ("lat_0", "lat_1")
MESH = pl.DeviceIdType.MESH

norm_eps = 1e-05
shrink_level = 0.01

F32 = jnp.float32
BF16 = jnp.bfloat16

N_LAT = 16
BAND = 24
CHN = 96
ROWS = CHN * BAND
LON = 768
LATS = N_LAT * BAND
CHUNKS = 3
KL = 8
ALL_CH = 768
PIECE = 12 * BAND

ORDER = [
    (1, 1), (3, 3), (2, 2), (1, 0), (3, 0), (0, 1), (0, 3), (1, 3), (3, 1),
    (2, 0), (0, 2), (1, 2), (3, 2), (2, 1), (2, 3),
]
CH_ORDER = [(1, 0), (3, 0), (1, 1), (3, 1), (2, 0), (2, 1), (0, 1)]


NSUB = 3
SUBSTEPS = 6 // NSUB
SUBROWS = PIECE // NSUB


def trig(length, n, f):
    ang = (n * f % length) * (2.0 * math.pi / length)
    scale = 1.0 / math.sqrt(length)
    return np.cos(ang) * scale, np.sin(ang) * scale


def lon_table():
    row = np.arange(LON)
    kk = row // 8 % 16
    q = row // 128 % 2 * 8 + row % 8
    mode = q * BAND + row // 256 * KL + kk % KL
    cs, sn = trig(LON, mode[:, None], np.arange(LON)[None, :])
    return np.where((kk < KL)[:, None], cs, -sn).reshape(CHUNKS, 256, LON).astype(BF16)


def lat_tables():
    n = np.arange(LATS)
    cs, sn = trig(LATS, n[:, None], n[None, :])
    return np.stack([cs, sn]).astype(BF16)


def area_table():
    row = np.arange(LATS, dtype=np.float32).reshape(N_LAT, BAND, 1)
    area = np.cos((row + 0.5) * (math.pi / LATS) - 0.5 * math.pi)
    return np.broadcast_to(area, (N_LAT, BAND, 128)).astype(np.float32)


def kernel(
    x_hbm, tb_hbm, cs_hbm, w1_ref, b_ref, w2_ref, area_ref, gain_ref, shift_ref,
    o_ref,
    X, TB, CS, V, N, TF, TI, LF, LI, SF, RF, SB, RB, G, R, SP, MX, AW, A1, A2, BT, B1,
    PS, ST, RS, RED, AG, AF, ES, EB, TC, EN, MI,
    xs, ts, fs, fr, bs, br, rss, rsr, ags, agr, afs, afr, es, er,
):
    y = lax.axis_index("lat_0")
    z = lax.axis_index("lat_1")
    cx = lax.axis_index("ch_0")
    ck = lax.axis_index("ch_1")
    me = y * 4 + z
    mc = cx * 2 + ck

    def x_copy(i):
        rows = pl.ds(pl.multiple_of(i * 384, 384), 384)
        return pltpu.make_async_copy(x_hbm.at[rows], X.at[rows], xs.at[i])

    for i in range(6):
        x_copy(i).start()
    pltpu.make_async_copy(tb_hbm, TB, ts.at[0]).start()
    pltpu.make_async_copy(cs_hbm, CS, ts.at[1]).start()

    def lat_to(a, b):
        yy = lax.rem(y + a, 4)
        zz = lax.rem(z + b, 4)
        return {"lat_0": yy, "lat_1": zz}, yy * 4 + zz

    def ch_to(a, b):
        xx = lax.rem(cx + a, 4)
        kk = lax.rem(ck + b, 2)
        return {"ch_0": xx, "ch_1": kk}, xx * 2 + kk

    bar = pltpu.get_barrier_semaphore()
    for a, b in ORDER:
        pl.semaphore_signal(bar, 1, device_id=lat_to(a, b)[0], device_id_type=MESH)
    for a, b in CH_ORDER:
        pl.semaphore_signal(bar, 1, device_id=ch_to(a, b)[0], device_id_type=MESH)

    def rcopy(src, dst, ss, rr, dev):
        return pltpu.make_async_remote_copy(
            src_ref=src, dst_ref=dst, send_sem=ss, recv_sem=rr, device_id=dev, device_id_type=MESH
        )

    def unit_start(sb, rb, ss, rr, c, u):
        for a, b in ORDER:
            dev, q = lat_to(a, b)
            rcopy(sb.at[c, u, q], rb.at[c, u, me], ss.at[c, u], rr.at[c, u], dev).start()
        rb[c, u, me] = sb[c, u, me]

    def unit_whole(sb, rb, ss, rr, c, u):
        peers = pl.ds(0, N_LAT - 1)
        dev = lat_to(1, 0)[0]
        return rcopy(sb.at[c, u, peers], rb.at[c, u, peers], ss.at[c, u], rr.at[c, u], dev)

    def stats_out():
        e = jnp.zeros((8, 128), F32)
        for hb in range(3):
            for lb in range(6):
                t = hb * 6 + lb
                rows, lanes = slice(8 * hb, 8 * hb + 8), slice(128 * lb, 128 * lb + 128)
                sq = PS[1, rows, lanes]
                ST[t] = PS[0, rows, lanes]
                ST[18 + t] = sq
                e = e + sq * area_ref[me, rows, :]
        ES[...] = e

    def e_copy(a, b):
        dev, q = lat_to(a, b)
        return rcopy(ES, EB.at[me], es.at[q], er.at[me], dev)

    def e_from(a, b):
        dev, p = lat_to(4 - a, 4 - b)
        return rcopy(ES, EB.at[p], es.at[p], er.at[p], dev)

    def rs_copy(a, b):
        dev, d = ch_to(a, b)
        return rcopy(ST.at[pl.ds(5 * d, 5)], RS.at[mc], rss.at[d], rsr.at[mc], dev)

    def rs_from(a, b):
        dev, d = ch_to(4 - a, 2 - b)
        return rcopy(ST.at[pl.ds(5 * d, 5)], RS.at[d], rss.at[d], rsr.at[d], dev)

    def ag_copy(a, b, part):
        dev, d = ch_to(a, b)
        return rcopy(RED.at[part], AG.at[mc, part], ags.at[d], agr.at[mc], dev)

    def ag_from(a, b, part):
        dev, d = ch_to(4 - a, 2 - b)
        return rcopy(RED.at[part], AG.at[d, part], ags.at[d], agr.at[d], dev)

    def rs_start():
        for a, b in CH_ORDER:
            rs_copy(a, b).start()
        RS[mc] = ST[pl.ds(5 * mc, 5)]

    def e_start():
        for a, b in ORDER:
            e_copy(a, b).start()
        EB[me] = ES[...]

    def rs_sum():
        for a, b in CH_ORDER:
            rs_from(a, b).wait_recv()
        tot = RS[0]
        for d in range(1, 8):
            tot = tot + RS[d]
        RED[0:5] = tot

    def e_sum():
        for a, b in ORDER:
            e_from(a, b).wait_recv()
        e = EB[0]
        for p in range(1, N_LAT):
            e = e + EB[p]
        return e

    def ag_start(part):
        for a, b in CH_ORDER:
            ag_copy(a, b, part).start()
        AG[mc, part] = RED[part]

    def ag_wait(part):
        for a, b in CH_ORDER:
            ag_from(a, b, part).wait_recv()

    def rs_sent():
        for a, b in CH_ORDER:
            rs_copy(a, b).wait_send()

    def ag_sent(part):
        for a, b in CH_ORDER:
            ag_copy(a, b, part).wait_send()

    def e_sent():
        for a, b in ORDER:
            e_copy(a, b).wait_send()

    def af_copy(a, b):
        dev, d = ch_to(a, b)
        return rcopy(RED.at[5], AF.at[mc], afs.at[d], afr.at[mc], dev)

    def af_from(a, b):
        dev, d = ch_to(4 - a, 2 - b)
        return rcopy(RED.at[5], AF.at[d], afs.at[d], afr.at[d], dev)

    def over_channels(tiles):
        e = tiles[0]
        for d in range(1, 8):
            e = e + tiles[d]
        e = jnp.sum(e, axis=0, keepdims=True)
        e = jnp.sum(e, axis=1, keepdims=True)
        return jnp.broadcast_to(e, (8, 128))

    def lane_masks():
        lane = lax.broadcasted_iota(jnp.int32, (48, 128), 1) & 7
        return [lane == s for s in range(8)]

    def block_swap(parts, masks):
        rolled = [p if r == 0 else pltpu.roll(p, r, 1) for r, p in enumerate(parts)]
        out = []
        for q in range(8):
            acc = rolled[-q % 8]
            for s in range(1, 8):
                acc = jnp.where(masks[s], rolled[(s - q) % 8], acc)
            out.append(acc if q == 0 else pltpu.roll(acc, 128 - q, 1))
        return out

    def rows_of(ii):
        return pl.ds(pl.multiple_of(ii * 48, 48), 48)

    def forward_step(c, u, ii):
        base = pl.multiple_of((u * SUBSTEPS + ii) * 384, 384)
        R[...] = jnp.dot(N[pl.ds(base, 384), :], TF[c], preferred_element_type=F32)
        masks = lane_masks()
        for half in range(2):
            hs = slice(128 * half, 128 * half + 128)
            parts = [
                jnp.concatenate(
                    [R[24 * r : 24 * r + 24, hs], R[192 + 24 * r : 216 + 24 * r, hs]], axis=0
                )
                for r in range(8)
            ]
            for q, piece in enumerate(block_swap(parts, masks)):
                SF[c, u, 8 * half + q, rows_of(ii), :] = piece.astype(BF16)

    def normalize_step(l, srow, i):
        def pair(j, _):
            base = i * 384 + j * 48
            ch = i * 16 + j * 2
            for lb in range(2):
                ls = slice(384 * lb, 384 * lb + 384)
                mean = MI[0, :, ls]
                inv = MI[1, :, ls]
                both = []
                for t in range(2):
                    rows = pl.ds(pl.multiple_of(base + 24 * t, 24), 24)
                    cur = (V[rows, ls] * srow).astype(BF16).astype(F32)
                    nrm = (cur - mean) * inv * gain_ref[l, ch + t] + shift_ref[l, ch + t]
                    nrm = nrm.astype(BF16).astype(F32)
                    V[rows, ls] = cur + nrm
                    both.append(nrm)
                N[pl.ds(pl.multiple_of(base, 48), 48), ls] = jnp.concatenate(both, axis=0).astype(BF16)
            return 0

        lax.fori_loop(0, 8, pair, 0)

    def forward_first(l, srow):
        def unit(u, _):
            def step(ii, _):
                normalize_step(l, srow, u * SUBSTEPS + ii)
                forward_step(0, u, ii)
                return 0

            lax.fori_loop(0, SUBSTEPS, step, 0)
            unit_start(SF, RF, fs, fr, 0, u)
            return 0

        lax.fori_loop(0, NSUB, unit, 0)

    def forward_rest():
        def unit(n, _):
            c = n // NSUB
            u = n % NSUB

            def step(ii, _):
                forward_step(c, u, ii)
                return 0

            lax.fori_loop(0, SUBSTEPS, step, 0)
            unit_start(SF, RF, fs, fr, c, u)
            return 0

        lax.fori_loop(NSUB, CHUNKS * NSUB, unit, 0)

    def middle_chunk(l, c):
        def gather_unit(u, _):
            unit_whole(SF, RF, fs, fr, c, u).wait_recv()

            def gather(ii, _):
                i = u * SUBSTEPS + ii
                got = [RF[c, u, p, rows_of(ii), :].astype(F32) for p in range(N_LAT)]
                for j in range(2):
                    blk = jnp.concatenate([g[24 * j : 24 * j + 24] for g in got], axis=0)
                    t = blk.T.reshape(16, 8, LATS)
                    G[:, pl.ds(pl.multiple_of(i * 16 + 8 * j, 8), 8), :] = t
                return 0

            lax.fori_loop(0, SUBSTEPS, gather, 0)
            return 0

        lax.fori_loop(0, NSUB, gather_unit, 0)

        def mix(b, _):
            g_re = G[pl.ds(4 * b, 4)].reshape(384, LATS).astype(BF16)
            g_im = G[pl.ds(8 + 4 * b, 4)].reshape(384, LATS).astype(BF16)
            SP[...] = jnp.dot(
                jnp.concatenate([g_re, g_im], axis=1), LF[...], preferred_element_type=F32
            ).astype(BF16)
            bias = jnp.concatenate([B1[l]] * 3, axis=1)
            for k in range(4):
                rows = slice(96 * k, 96 * k + 96)
                both = jnp.concatenate([SP[rows, 0:LATS], SP[rows, LATS:]], axis=0)
                hid = jnp.dot(A1[l], both, preferred_element_type=F32) + bias
                hid = jnp.maximum(hid, 0.0).astype(BF16)
                m = jnp.dot(A2[l], hid, preferred_element_type=F32)
                m = (m - jnp.clip(m, -shrink_level, shrink_level)).astype(BF16)
                MX[rows, 0:LATS] = m[0:96]
                MX[rows, LATS:] = m[96:192]
            back = jnp.dot(MX[...], LI[...], preferred_element_type=F32)
            G[pl.ds(4 * b, 4)] = back[:, 0:LATS].reshape(4, CHN, LATS)
            G[pl.ds(8 + 4 * b, 4)] = back[:, LATS:].reshape(4, CHN, LATS)
            return 0

        lax.fori_loop(0, 2, mix, 0)

        def scatter_unit(u, _):
            def scatter(ii, _):
                i = u * SUBSTEPS + ii
                ts = []
                for j in range(2):
                    blk = G[:, pl.ds(pl.multiple_of(i * 16 + 8 * j, 8), 8), :].reshape(128, LATS)
                    ts.append(blk.T)
                for p in range(N_LAT):
                    piece = jnp.concatenate([t[24 * p : 24 * p + 24] for t in ts], axis=0)
                    SB[c, u, p, rows_of(ii), :] = piece.astype(BF16)
                return 0

            lax.fori_loop(0, SUBSTEPS, scatter, 0)
            unit_start(SB, RB, bs, br, c, u)
            return 0

        lax.fori_loop(0, NSUB, scatter_unit, 0)

    def backward_unit(c, u, last):
        unit_whole(SB, RB, bs, br, c, u).wait_recv()

        def step(ii, _):
            masks = lane_masks()
            for half in range(2):
                hs = slice(128 * half, 128 * half + 128)
                parts = [RB[c, u, 8 * half + q, rows_of(ii), :].astype(F32) for q in range(8)]
                for r, piece in enumerate(block_swap(parts, masks)):
                    R[24 * r : 24 * r + 24, hs] = piece[0:24]
                    R[192 + 24 * r : 216 + 24 * r, hs] = piece[24:48]
            rows = pl.ds(pl.multiple_of((u * SUBSTEPS + ii) * 384, 384), 384)
            v = V[rows, :] + jnp.dot(R[...].astype(BF16), TI[c], preferred_element_type=F32)
            V[rows, :] = v
            if last:
                v = v.reshape(16, BAND, LON)
                PS[0] += jnp.sum(v, axis=0)
                PS[1] += jnp.sum(v * v, axis=0)
            return 0

        lax.fori_loop(0, SUBSTEPS, step, 0)

    def set_tables():
        pltpu.make_async_copy(tb_hbm, TB, ts.at[0]).wait()
        pltpu.make_async_copy(cs_hbm, CS, ts.at[1]).wait()
        row = lax.broadcasted_iota(jnp.int32, (256, LON), 0)
        for c in range(CHUNKS):
            t = TB[c].astype(F32)
            TF[c] = t.T.astype(BF16)
            twice = t * 2.0
            TI[c] = (jnp.where(row == 0, t, twice) if c == 0 else twice).astype(BF16)
        cl = CS[0]
        sl = CS[1]
        LF[0:LATS, 0:LATS] = cl
        LF[0:LATS, LATS:] = -sl
        LF[LATS:, 0:LATS] = sl
        LF[LATS:, LATS:] = cl
        LI[0:LATS, 0:LATS] = cl
        LI[0:LATS, LATS:] = sl
        LI[LATS:, 0:LATS] = -sl
        LI[LATS:, LATS:] = cl
        AW[...] = jnp.zeros((256, 256), F32)
        BT[...] = jnp.zeros((128, 128), F32)
        for l in range(2):
            for w_ref, a_ref in ((w1_ref, A1), (w2_ref, A2)):
                re = w_ref[l, 0].astype(F32)
                im = w_ref[l, 1].astype(F32)
                AW[0:96, 0:192] = jnp.concatenate([re, im], axis=1)
                AW[96:192, 0:192] = jnp.concatenate([-im, re], axis=1)
                a_ref[l] = AW[...].T[0:192, 0:192].astype(BF16)
            for part in range(2):
                BT[:, 0:96] = jnp.broadcast_to(b_ref[l, part : part + 1, :].astype(F32), (128, 96))
                B1[l, 96 * part : 96 * part + 96, :] = BT[...].T[0:96, :]

    def set_mean_inv(scale):
        for hb in range(3):
            for lb in range(6):
                t = hb * 6 + lb
                u = t + 18
                mean = AG[t // 5, t % 5] * scale * (1.0 / ALL_CH)
                spread = AG[u // 5, u % 5] * (scale * scale) * (1.0 / ALL_CH) - mean * mean
                MI[0, 8 * hb : 8 * hb + 8, 128 * lb : 128 * lb + 128] = mean
                MI[1, 8 * hb : 8 * hb + 8, 128 * lb : 128 * lb + 128] = lax.rsqrt(spread + norm_eps)

    five, seven = pl.ds(0, 5), pl.ds(0, 7)

    zero = jnp.zeros((BAND, LON), F32)
    for t in range(36, 40):
        ST[t] = jnp.zeros((8, 128), F32)

    def first_block(i, carry):
        x_copy(i).wait()

        def pair(j, carry):
            s1, s2 = carry
            rows = pl.ds(pl.multiple_of(i * 384 + j * 48, 48), 48)
            xx = X[rows, :].astype(F32)
            V[rows, :] = xx
            for t in range(2):
                v = xx[24 * t : 24 * t + 24]
                s1 = s1 + v
                s2 = s2 + v * v
            return s1, s2

        return lax.fori_loop(0, 8, pair, carry)

    s1, s2 = lax.fori_loop(0, 6, first_block, (zero, zero))
    PS[0] = s1
    PS[1] = s2
    stats_out()
    pl.semaphore_wait(bar, len(ORDER) + len(CH_ORDER))
    rs_start()
    e_start()
    set_tables()
    rs_sum()
    ag_start(five)
    TC[...] = e_sum()
    ag_wait(five)
    rs_sent()
    ag_sent(five)
    e_sent()

    def layer(l, scale):
        set_mean_inv(scale)
        srow = scale[0:1, 0:1]
        forward_first(l, srow)
        forward_rest()

        def mid(c, _):
            middle_chunk(l, c)
            return 0

        lax.fori_loop(0, CHUNKS, mid, 0)

        def back(n, _):
            backward_unit(n // NSUB, n % NSUB, False)
            return 0

        lax.fori_loop(0, (CHUNKS - 1) * NSUB, back, 0)
        PS[...] = jnp.zeros((2, BAND, LON), F32)

        def back_last(u, _):
            backward_unit(CHUNKS - 1, u, True)
            return 0

        lax.fori_loop(0, NSUB, back_last, 0)
        stats_out()
        e_start()

        @pl.when(l == 0)
        def _():
            rs_start()
            rs_sum()
            RED[6] = TC[...]
            RED[5] = e_sum()
            ag_start(seven)
            ag_wait(seven)
            TC[...] = over_channels([AG[d, 6] for d in range(8)])
            EN[...] = over_channels([AG[d, 5] for d in range(8)])
            rs_sent()
            ag_sent(seven)

        @pl.when(l == 1)
        def _():
            RED[5] = e_sum()
            for a, b in CH_ORDER:
                af_copy(a, b).start()
            AF[mc] = RED[5]
            for a, b in CH_ORDER:
                af_from(a, b).wait_recv()
            EN[...] = over_channels([AF[d] for d in range(8)])
            for a, b in CH_ORDER:
                af_copy(a, b).wait_send()

        e_sent()

        def sent(n, _):
            c = n // NSUB
            u = n % NSUB
            unit_whole(SF, RF, fs, fr, c, u).wait_send()
            unit_whole(SB, RB, bs, br, c, u).wait_send()
            return 0

        lax.fori_loop(0, CHUNKS * NSUB, sent, 0)
        return jnp.sqrt(TC[...] / EN[...])

    scale = lax.fori_loop(0, 2, layer, jnp.ones((8, 128), F32))
    srow = scale[0:1, 0:1]

    def finish(i, _):
        rows = pl.ds(pl.multiple_of(i * 96, 96), 96)
        o_ref[rows, :] = (V[rows, :] * srow).astype(BF16)
        return 0

    lax.fori_loop(0, ROWS // 96, finish, 0)


def per_device(field_in, ln_gain, ln_shift, mix_first, mix_bias, mix_second):
    vm = pl.BlockSpec(memory_space=pltpu.VMEM)
    sm = pl.BlockSpec(memory_space=pltpu.SMEM)
    hbm = pl.BlockSpec(memory_space=pl.ANY)
    dma = pltpu.SemaphoreType.DMA
    buf = pltpu.VMEM((CHUNKS, NSUB, N_LAT, SUBROWS, 128), BF16)
    unit = dma((CHUNKS, NSUB))
    out = pl.pallas_call(
        kernel,
        out_shape=jax.ShapeDtypeStruct((ROWS, LON), BF16),
        in_specs=[hbm] * 3 + [vm] * 4 + [sm] * 2,
        out_specs=vm,
        scratch_shapes=[
            pltpu.VMEM((ROWS, LON), BF16),
            pltpu.VMEM((CHUNKS, 256, LON), BF16),
            pltpu.VMEM((2, LATS, LATS), BF16),
            pltpu.VMEM((ROWS, LON), F32),
            pltpu.VMEM((ROWS, LON), BF16),
            pltpu.VMEM((CHUNKS, LON, 256), BF16),
            pltpu.VMEM((CHUNKS, 256, LON), BF16),
            pltpu.VMEM((2 * LATS, 2 * LATS), BF16),
            pltpu.VMEM((2 * LATS, 2 * LATS), BF16),
            buf,
            buf,
            buf,
            buf,
            pltpu.VMEM((16, CHN, LATS), F32),
            pltpu.VMEM((384, 256), F32),
            pltpu.VMEM((384, 2 * LATS), BF16),
            pltpu.VMEM((384, 2 * LATS), BF16),
            pltpu.VMEM((256, 256), F32),
            pltpu.VMEM((2, 192, 192), BF16),
            pltpu.VMEM((2, 192, 192), BF16),
            pltpu.VMEM((128, 128), F32),
            pltpu.VMEM((2, 192, 128), F32),
            pltpu.VMEM((2, BAND, LON), F32),
            pltpu.VMEM((40, 8, 128), F32),
            pltpu.VMEM((8, 5, 8, 128), F32),
            pltpu.VMEM((7, 8, 128), F32),
            pltpu.VMEM((8, 7, 8, 128), F32),
            pltpu.VMEM((8, 8, 128), F32),
            pltpu.VMEM((8, 128), F32),
            pltpu.VMEM((N_LAT, 8, 128), F32),
            pltpu.VMEM((8, 128), F32),
            pltpu.VMEM((8, 128), F32),
            pltpu.VMEM((2, BAND, LON), F32),
            dma((6,)),
            dma((2,)),
            unit,
            unit,
            unit,
            unit,
            dma((8,)),
            dma((8,)),
            dma((8,)),
            dma((8,)),
            dma((8,)),
            dma((8,)),
            dma((N_LAT,)),
            dma((N_LAT,)),
        ],
        compiler_params=pltpu.CompilerParams(
            collective_id=0, has_side_effects=True, vmem_limit_bytes=60 * 1024 * 1024
        ),
    )(
        field_in.reshape(ROWS, LON), lon_table(), lat_tables(), mix_first[:, :, 0], mix_bias[:, :, 0],
        mix_second[:, :, 0], area_table(), ln_gain, ln_shift,
    )
    return out.reshape(CHN, BAND, LON)


def solution(mesh):
    finer = Mesh(mesh.devices.reshape(4, 4, 4, 2), ("lat_0", "lat_1", "ch_0", "ch_1"))
    in_specs = (
        P(CH, LAT, None),
        P(None, CH),
        P(None, CH),
        P(None, None, CH, None, None),
        P(None, None, CH, None),
        P(None, None, CH, None, None),
    )
    return jax.shard_map(
        per_device, mesh=finer, in_specs=in_specs, out_specs=P(CH, LAT, None), check_vma=False
    )
```

time: 255 us -> 211 us (0.83)
  Pallas kernels: 230 us -> 207 us
  other arithmetic: 15.9 us -> 0 us
  local copies, waits for them, and re-layouts: 8.24 us -> 4.02 us
    pallas_call x1, Pallas kernels: 230 us -> 207 us  [per_device(): pl.pallas_call(kernel, out_shape=jax.ShapeDtypeStruct((ROWS, LON), BF16),...]
    convert_element_type x2 -> x0, other arithmetic: 14.9 us -> none  [the longest x1 11.6 us: lon_table(): jnp.where((kk < KL)[:, None], cs, -sn).astype(BF16)]
    unnamed x3 -> x1, local copies, waits for them, and re-layouts: 6.01 us -> 4.02 us
where the time goes in v2:
time: 211 us
  Pallas kernels  207 us (98%)
  local copies, waits for them, and re-layouts  4.02 us (2%)
    pallas_call x1, Pallas kernels, per_device(): pl.pallas_call(kernel, out_shape=jax.ShapeDtypeStruct((ROWS, LON), BF16),...  207 us

profile of v2, /device:TPU:1, one launch (start us, length us, event | category | flops | bytes accessed | tf_op | source)
XLA Modules:
  0.0 210.6 jit_solution(15583200687071715970)
XLA Ops:
  0.0 206.6 %shard_map.91 = bf16[2304,768]{1,0:T(8,128)(2,1)} custom-call(bf16[2304,768]{1,0:T(8,128)(2,1)} %bitcast.6, bf16[3,256,768]{2,1,0:T(8,128)(2,1)} %constant.6.clone.tb_hbm, bf16[2,384,384]{2,1,0:T(8,128)(2,1)} %constant.7.clone.cs_hbm, bf16[2,2,96,96]{3,2,1,0:T(8,128)(2,1)} %bitcast.7, bf16[2,2,96]{2,1,0:T(2,128)(2,1)} %bitcast.9, ...), custom_call_target="tpu_custom_call" | custom-call | tf_op jit(solution)/shard_map/pallas_call | solution.py:550
  206.6 4.0 %copy.11 = bf16[96,24,768]{2,1,0:T(8,128)(2,1)} copy(bf16[96,24,768]{2,1,0:T(8,128)(2,1)} %bitcast.5) | data formatting | bytes 7077888

commit v3 on v2

--- a/solution.py
+++ b/solution.py
@@ -31,13 +31,13 @@
 PIECE = 12 * BAND
 
 ORDER = [
-    (1, 1), (3, 3), (2, 2), (1, 0), (3, 0), (0, 1), (0, 3), (1, 3), (3, 1),
-    (2, 0), (0, 2), (1, 2), (3, 2), (2, 1), (2, 3),
+    (2, 2), (1, 2), (2, 1), (2, 3), (3, 2), (0, 2), (1, 1), (1, 3), (2, 0),
+    (3, 1), (3, 3), (0, 1), (0, 3), (1, 0), (3, 0),
 ]
 CH_ORDER = [(1, 0), (3, 0), (1, 1), (3, 1), (2, 0), (2, 1), (0, 1)]
 
 
-NSUB = 3
+NSUB = 6
 SUBSTEPS = 6 // NSUB
 SUBROWS = PIECE // NSUB
 
@@ -70,11 +70,11 @@
 
 
 def kernel(
-    x_hbm, tb_hbm, cs_hbm, w1_ref, b_ref, w2_ref, area_ref, gain_ref, shift_ref,
-    o_ref,
-    X, TB, CS, V, N, TF, TI, LF, LI, SF, RF, SB, RB, G, R, SP, MX, AW, A1, A2, BT, B1,
-    PS, ST, RS, RED, AG, AF, ES, EB, TC, EN, MI,
-    xs, ts, fs, fr, bs, br, rss, rsr, ags, agr, afs, afr, es, er,
+    x_hbm, tb_hbm, cs_hbm, w1_hbm, b_hbm, w2_hbm, area_hbm, gain_hbm, shift_hbm,
+    o_hbm, SC,
+    X, TB, CS, w1_ref, b_ref, w2_ref, area_ref, gain_ref, shift_ref, V, N, TF, TI, LF, LI, SF, RF, SB, RB, G, R, SP, MX, AW, A1, A2, BT, B1,
+    PS, ST, RS, RED, AG, EX, AE, AT, AF, ES, EB, TC, EN, MI,
+    xs, ts, os, fs, fr, bs, br, rss, rsr, ags, agr, aes, aer, ats, atr, afs, afr, es, er,
 ):
     y = lax.axis_index("lat_0")
     z = lax.axis_index("lat_1")
@@ -89,8 +89,23 @@
 
     for i in range(6):
         x_copy(i).start()
-    pltpu.make_async_copy(tb_hbm, TB, ts.at[0]).start()
-    pltpu.make_async_copy(cs_hbm, CS, ts.at[1]).start()
+    small = [
+        pltpu.make_async_copy(src, dst, ts.at[n])
+        for n, (src, dst) in enumerate(
+            (
+                (area_hbm.at[me], area_ref),
+                (tb_hbm, TB),
+                (cs_hbm, CS),
+                (w1_hbm, w1_ref),
+                (b_hbm, b_ref),
+                (w2_hbm, w2_ref),
+                (gain_hbm, gain_ref),
+                (shift_hbm, shift_ref),
+            )
+        )
+    ]
+    for copy in small:
+        copy.start()
 
     def lat_to(a, b):
         yy = lax.rem(y + a, 4)
@@ -133,8 +148,8 @@
                 sq = PS[1, rows, lanes]
                 ST[t] = PS[0, rows, lanes]
                 ST[18 + t] = sq
-                e = e + sq * area_ref[me, rows, :]
-        ES[...] = e
+                e = e + sq * area_ref[rows, :]
+        ES[...] = jnp.sum(e, axis=0, keepdims=True)
 
     def e_copy(a, b):
         dev, q = lat_to(a, b)
@@ -152,13 +167,13 @@
         dev, d = ch_to(4 - a, 2 - b)
         return rcopy(ST.at[pl.ds(5 * d, 5)], RS.at[d], rss.at[d], rsr.at[d], dev)
 
-    def ag_copy(a, b, part):
+    def ag_copy(a, b):
         dev, d = ch_to(a, b)
-        return rcopy(RED.at[part], AG.at[mc, part], ags.at[d], agr.at[mc], dev)
-
-    def ag_from(a, b, part):
+        return rcopy(RED, AG.at[mc], ags.at[d], agr.at[mc], dev)
+
+    def ag_from(a, b):
         dev, d = ch_to(4 - a, 2 - b)
-        return rcopy(RED.at[part], AG.at[d, part], ags.at[d], agr.at[d], dev)
+        return rcopy(RED, AG.at[d], ags.at[d], agr.at[d], dev)
 
     def rs_start():
         for a, b in CH_ORDER:
@@ -176,7 +191,7 @@
         tot = RS[0]
         for d in range(1, 8):
             tot = tot + RS[d]
-        RED[0:5] = tot
+        RED[...] = tot
 
     def e_sum():
         for a, b in ORDER:
@@ -186,40 +201,53 @@
             e = e + EB[p]
         return e
 
-    def ag_start(part):
-        for a, b in CH_ORDER:
-            ag_copy(a, b, part).start()
-        AG[mc, part] = RED[part]
-
-    def ag_wait(part):
-        for a, b in CH_ORDER:
-            ag_from(a, b, part).wait_recv()
+    def ag_start():
+        for a, b in CH_ORDER:
+            ag_copy(a, b).start()
+        AG[mc] = RED[...]
+
+    def ag_wait():
+        for a, b in CH_ORDER:
+            ag_from(a, b).wait_recv()
 
     def rs_sent():
         for a, b in CH_ORDER:
             rs_copy(a, b).wait_send()
 
-    def ag_sent(part):
-        for a, b in CH_ORDER:
-            ag_copy(a, b, part).wait_send()
+    def ag_sent():
+        for a, b in CH_ORDER:
+            ag_copy(a, b).wait_send()
 
     def e_sent():
         for a, b in ORDER:
             e_copy(a, b).wait_send()
 
-    def af_copy(a, b):
+    def row_copy(n, dst, ss, rr, a, b):
         dev, d = ch_to(a, b)
-        return rcopy(RED.at[5], AF.at[mc], afs.at[d], afr.at[mc], dev)
-
-    def af_from(a, b):
+        return rcopy(EX.at[n], dst.at[mc], ss.at[d], rr.at[mc], dev)
+
+    def row_from(n, dst, ss, rr, a, b):
         dev, d = ch_to(4 - a, 2 - b)
-        return rcopy(RED.at[5], AF.at[d], afs.at[d], afr.at[d], dev)
+        return rcopy(EX.at[n], dst.at[d], ss.at[d], rr.at[d], dev)
+
+    def row_start(n, dst, ss, rr):
+        for a, b in CH_ORDER:
+            row_copy(n, dst, ss, rr, a, b).start()
+        dst[mc] = EX[n]
+
+    def row_sum(n, dst, ss, rr):
+        for a, b in CH_ORDER:
+            row_from(n, dst, ss, rr, a, b).wait_recv()
+        return over_channels([dst[d] for d in range(8)])
+
+    def row_sent(n, dst, ss, rr):
+        for a, b in CH_ORDER:
+            row_copy(n, dst, ss, rr, a, b).wait_send()
 
     def over_channels(tiles):
         e = tiles[0]
         for d in range(1, 8):
             e = e + tiles[d]
-        e = jnp.sum(e, axis=0, keepdims=True)
         e = jnp.sum(e, axis=1, keepdims=True)
         return jnp.broadcast_to(e, (8, 128))
 
@@ -363,7 +391,11 @@
 
         lax.fori_loop(0, NSUB, scatter_unit, 0)
 
-    def backward_unit(c, u, last):
+    def o_copy(i):
+        rows = pl.ds(pl.multiple_of(i * 384, 384), 384)
+        return pltpu.make_async_copy(X.at[rows], o_hbm.at[rows], os.at[i])
+
+    def backward_unit(l, c, u, last):
         unit_whole(SB, RB, bs, br, c, u).wait_recv()
 
         def step(ii, _):
@@ -378,6 +410,12 @@
             v = V[rows, :] + jnp.dot(R[...].astype(BF16), TI[c], preferred_element_type=F32)
             V[rows, :] = v
             if last:
+                X[rows, :] = v.astype(BF16)
+
+                @pl.when(l == 1)
+                def _():
+                    o_copy(u * SUBSTEPS + ii).start()
+
                 v = v.reshape(16, BAND, LON)
                 PS[0] += jnp.sum(v, axis=0)
                 PS[1] += jnp.sum(v * v, axis=0)
@@ -386,8 +424,8 @@
         lax.fori_loop(0, SUBSTEPS, step, 0)
 
     def set_tables():
-        pltpu.make_async_copy(tb_hbm, TB, ts.at[0]).wait()
-        pltpu.make_async_copy(cs_hbm, CS, ts.at[1]).wait()
+        for copy in small[1:]:
+            copy.wait()
         row = lax.broadcasted_iota(jnp.int32, (256, LON), 0)
         for c in range(CHUNKS):
             t = TB[c].astype(F32)
@@ -427,7 +465,9 @@
                 MI[0, 8 * hb : 8 * hb + 8, 128 * lb : 128 * lb + 128] = mean
                 MI[1, 8 * hb : 8 * hb + 8, 128 * lb : 128 * lb + 128] = lax.rsqrt(spread + norm_eps)
 
-    five, seven = pl.ds(0, 5), pl.ds(0, 7)
+    by_energy = (0, AE, aes, aer)
+    by_target = (1, AT, ats, atr)
+    by_last = (0, AF, afs, afr)
 
     zero = jnp.zeros((BAND, LON), F32)
     for t in range(36, 40):
@@ -452,17 +492,18 @@
     s1, s2 = lax.fori_loop(0, 6, first_block, (zero, zero))
     PS[0] = s1
     PS[1] = s2
+    small[0].wait()
     stats_out()
     pl.semaphore_wait(bar, len(ORDER) + len(CH_ORDER))
     rs_start()
     e_start()
     set_tables()
     rs_sum()
-    ag_start(five)
-    TC[...] = e_sum()
-    ag_wait(five)
+    ag_start()
+    EX[1] = e_sum()
+    ag_wait()
     rs_sent()
-    ag_sent(five)
+    ag_sent()
     e_sent()
 
     def layer(l, scale):
@@ -478,44 +519,43 @@
         lax.fori_loop(0, CHUNKS, mid, 0)
 
         def back(n, _):
-            backward_unit(n // NSUB, n % NSUB, False)
+            backward_unit(l, n // NSUB, n % NSUB, False)
             return 0
 
         lax.fori_loop(0, (CHUNKS - 1) * NSUB, back, 0)
         PS[...] = jnp.zeros((2, BAND, LON), F32)
 
         def back_last(u, _):
-            backward_unit(CHUNKS - 1, u, True)
+            backward_unit(l, CHUNKS - 1, u, True)
             return 0
 
         lax.fori_loop(0, NSUB, back_last, 0)
         stats_out()
-        e_start()
 
         @pl.when(l == 0)
         def _():
             rs_start()
+            e_start()
+            row_start(*by_target)
             rs_sum()
-            RED[6] = TC[...]
-            RED[5] = e_sum()
-            ag_start(seven)
-            ag_wait(seven)
-            TC[...] = over_channels([AG[d, 6] for d in range(8)])
-            EN[...] = over_channels([AG[d, 5] for d in range(8)])
+            ag_start()
+            EX[0] = e_sum()
+            row_start(*by_energy)
+            TC[...] = row_sum(*by_target)
+            ag_wait()
+            EN[...] = row_sum(*by_energy)
             rs_sent()
-            ag_sent(seven)
+            ag_sent()
+            row_sent(*by_target)
+            row_sent(*by_energy)
 
         @pl.when(l == 1)
         def _():
-            RED[5] = e_sum()
-            for a, b in CH_ORDER:
-                af_copy(a, b).start()
-            AF[mc] = RED[5]
-            for a, b in CH_ORDER:
-                af_from(a, b).wait_recv()
-            EN[...] = over_channels([AF[d] for d in range(8)])
-            for a, b in CH_ORDER:
-                af_copy(a, b).wait_send()
+            e_start()
+            EX[0] = e_sum()
+            row_start(*by_last)
+            EN[...] = row_sum(*by_last)
+            row_sent(*by_last)
 
         e_sent()
 
@@ -530,32 +570,59 @@
         return jnp.sqrt(TC[...] / EN[...])
 
     scale = lax.fori_loop(0, 2, layer, jnp.ones((8, 128), F32))
-    srow = scale[0:1, 0:1]
-
-    def finish(i, _):
-        rows = pl.ds(pl.multiple_of(i * 96, 96), 96)
-        o_ref[rows, :] = (V[rows, :] * srow).astype(BF16)
-        return 0
-
-    lax.fori_loop(0, ROWS // 96, finish, 0)
+    SC[...] = scale
+    for i in range(6):
+        o_copy(i).wait()
+
+
+def scale_kernel(v_hbm, s_hbm, o_hbm, vin, sin, vout, si, so, ss):
+    def rows(n):
+        return slice(192 * n, 192 * n + 192)
+
+    def come(n):
+        return pltpu.make_async_copy(v_hbm.at[rows(n)], vin.at[rows(n)], si.at[n])
+
+    def go(n):
+        return pltpu.make_async_copy(vout.at[rows(n)], o_hbm.at[rows(n)], so.at[n])
+
+    get_scale = pltpu.make_async_copy(s_hbm, sin, ss)
+    get_scale.start()
+    for n in range(12):
+        come(n).start()
+    get_scale.wait()
+    scale = sin[0:1, 0:1]
+    for n in range(12):
+        come(n).wait()
+        vout[rows(n), :] = (vin[rows(n), :].astype(F32) * scale).astype(BF16)
+        go(n).start()
+    for n in range(12):
+        go(n).wait()
 
 
 def per_device(field_in, ln_gain, ln_shift, mix_first, mix_bias, mix_second):
     vm = pl.BlockSpec(memory_space=pltpu.VMEM)
-    sm = pl.BlockSpec(memory_space=pltpu.SMEM)
     hbm = pl.BlockSpec(memory_space=pl.ANY)
     dma = pltpu.SemaphoreType.DMA
     buf = pltpu.VMEM((CHUNKS, NSUB, N_LAT, SUBROWS, 128), BF16)
     unit = dma((CHUNKS, NSUB))
-    out = pl.pallas_call(
+    summed, scale = pl.pallas_call(
         kernel,
-        out_shape=jax.ShapeDtypeStruct((ROWS, LON), BF16),
-        in_specs=[hbm] * 3 + [vm] * 4 + [sm] * 2,
-        out_specs=vm,
+        out_shape=(
+            jax.ShapeDtypeStruct((ROWS, LON), BF16),
+            jax.ShapeDtypeStruct((8, 128), F32),
+        ),
+        in_specs=[hbm] * 9,
+        out_specs=(hbm, vm),
         scratch_shapes=[
             pltpu.VMEM((ROWS, LON), BF16),
             pltpu.VMEM((CHUNKS, 256, LON), BF16),
             pltpu.VMEM((2, LATS, LATS), BF16),
+            pltpu.VMEM((2, 2, CHN, CHN), BF16),
+            pltpu.VMEM((2, 2, CHN), BF16),
+            pltpu.VMEM((2, 2, CHN, CHN), BF16),
+            pltpu.VMEM((BAND, 128), F32),
+            pltpu.SMEM((2, CHN), F32),
+            pltpu.SMEM((2, CHN), F32),
             pltpu.VMEM((ROWS, LON), F32),
             pltpu.VMEM((ROWS, LON), BF16),
             pltpu.VMEM((CHUNKS, LON, 256), BF16),
@@ -578,20 +645,28 @@
             pltpu.VMEM((2, BAND, LON), F32),
             pltpu.VMEM((40, 8, 128), F32),
             pltpu.VMEM((8, 5, 8, 128), F32),
-            pltpu.VMEM((7, 8, 128), F32),
-            pltpu.VMEM((8, 7, 8, 128), F32),
-            pltpu.VMEM((8, 8, 128), F32),
-            pltpu.VMEM((8, 128), F32),
-            pltpu.VMEM((N_LAT, 8, 128), F32),
+            pltpu.VMEM((5, 8, 128), F32),
+            pltpu.VMEM((8, 5, 8, 128), F32),
+            pltpu.VMEM((2, 1, 128), F32),
+            pltpu.VMEM((8, 1, 128), F32),
+            pltpu.VMEM((8, 1, 128), F32),
+            pltpu.VMEM((8, 1, 128), F32),
+            pltpu.VMEM((1, 128), F32),
+            pltpu.VMEM((N_LAT, 1, 128), F32),
             pltpu.VMEM((8, 128), F32),
             pltpu.VMEM((8, 128), F32),
             pltpu.VMEM((2, BAND, LON), F32),
             dma((6,)),
-            dma((2,)),
+            dma((8,)),
+            dma((6,)),
             unit,
             unit,
             unit,
             unit,
+            dma((8,)),
+            dma((8,)),
+            dma((8,)),
+            dma((8,)),
             dma((8,)),
             dma((8,)),
             dma((8,)),
@@ -608,6 +683,20 @@
         field_in.reshape(ROWS, LON), lon_table(), lat_tables(), mix_first[:, :, 0], mix_bias[:, :, 0],
         mix_second[:, :, 0], area_table(), ln_gain, ln_shift,
     )
+    out = pl.pallas_call(
+        scale_kernel,
+        out_shape=jax.ShapeDtypeStruct((ROWS, LON), BF16),
+        in_specs=[hbm, hbm],
+        out_specs=hbm,
+        scratch_shapes=[
+            pltpu.VMEM((ROWS, LON), BF16),
+            pltpu.VMEM((8, 128), F32),
+            pltpu.VMEM((ROWS, LON), BF16),
+            dma((12,)),
+            dma((12,)),
+            dma(()),
+        ],
+    )(summed, scale)
     return out.reshape(CHN, BAND, LON)
 
 

time: 211 us -> 202 us (0.957)
  Pallas kernels: 207 us -> 202 us
  local copies, waits for them, and re-layouts: 4.02 us -> 0 us
    pallas_call x1 -> x2, Pallas kernels: 207 us -> 202 us  [the longest x1 199 us: per_device(): pl.pallas_call(kernel, out_shape=(jax.ShapeDtypeStruct((ROWS, LON), BF16)...]
    unnamed x1 -> x0, local copies, waits for them, and re-layouts: 4.02 us -> none
where the time goes in v3:
time: 202 us
  Pallas kernels  202 us (100%)
    pallas_call x1, Pallas kernels, per_device(): pl.pallas_call(kernel, out_shape=(jax.ShapeDtypeStruct((ROWS, LON), BF16)...  199 us

profile of v3, /device:TPU:1, one launch (start us, length us, event | category | flops | bytes accessed | tf_op | source)
XLA Modules:
  0.0 202.4 jit_solution(6313880876239949177)
XLA Ops:
  0.0 198.6 %shard_map.91 = (bf16[2304,768]{1,0:T(8,128)(2,1)}, f32[8,128]{1,0:T(8,128)}) custom-call(bf16[2304,768]{1,0:T(8,128)(2,1)} %bitcast.5, bf16[3,256,768]{2,1,0:T(8,128)(2,1)} %constant.6.clone.tb_hbm, bf16[2,384,384]{2,1,0:T(8,128)(2,1)} %constant.7.clone.cs_hbm, bf16[2,2,96,96]{3,2,1,0:T(8,128)(2,1)} %bitcast.6, bf16[2,2,96]{2,1,0:T(2,128)(2,1)} %bitcast.8, ...), custom_call_target="tpu_custom_call" | custom-call | tf_op jit(solution)/shard_map/pallas_call | solution.py:608
  198.6 3.8 %shard_map.92 = bf16[2304,768]{1,0:T(8,128)(2,1)} custom-call(bf16[2304,768]{1,0:T(8,128)(2,1)} %get-tuple-element.7.v_hbm, f32[8,128]{1,0:T(8,128)} %get-tuple-element.8.s_hbm), custom_call_target="tpu_custom_call" | custom-call | tf_op jit(solution)/shard_map/pallas_call | solution.py:686

commit v4 on v3

--- a/solution.py
+++ b/solution.py
@@ -71,10 +71,10 @@
 
 def kernel(
     x_hbm, tb_hbm, cs_hbm, w1_hbm, b_hbm, w2_hbm, area_hbm, gain_hbm, shift_hbm,
-    o_hbm, SC,
-    X, TB, CS, w1_ref, b_ref, w2_ref, area_ref, gain_ref, shift_ref, V, N, TF, TI, LF, LI, SF, RF, SB, RB, G, R, SP, MX, AW, A1, A2, BT, B1,
+    V, SC,
+    X, TB, CS, w1_ref, b_ref, w2_ref, area_ref, gain_ref, shift_ref, N, TF, TI, LF, LI, SF, RF, SB, RB, G, R, SP, MX, AW, A1, A2, BT, B1,
     PS, ST, RS, RED, AG, EX, AE, AT, AF, ES, EB, TC, EN, MI,
-    xs, ts, os, fs, fr, bs, br, rss, rsr, ags, agr, aes, aer, ats, atr, afs, afr, es, er,
+    xs, ts, fs, fr, bs, br, rss, rsr, ags, agr, aes, aer, ats, atr, afs, afr, es, er,
 ):
     y = lax.axis_index("lat_0")
     z = lax.axis_index("lat_1")
@@ -391,10 +391,6 @@
 
         lax.fori_loop(0, NSUB, scatter_unit, 0)
 
-    def o_copy(i):
-        rows = pl.ds(pl.multiple_of(i * 384, 384), 384)
-        return pltpu.make_async_copy(X.at[rows], o_hbm.at[rows], os.at[i])
-
     def backward_unit(l, c, u, last):
         unit_whole(SB, RB, bs, br, c, u).wait_recv()
 
@@ -410,12 +406,6 @@
             v = V[rows, :] + jnp.dot(R[...].astype(BF16), TI[c], preferred_element_type=F32)
             V[rows, :] = v
             if last:
-                X[rows, :] = v.astype(BF16)
-
-                @pl.when(l == 1)
-                def _():
-                    o_copy(u * SUBSTEPS + ii).start()
-
                 v = v.reshape(16, BAND, LON)
                 PS[0] += jnp.sum(v, axis=0)
                 PS[1] += jnp.sum(v * v, axis=0)
@@ -571,29 +561,17 @@
 
     scale = lax.fori_loop(0, 2, layer, jnp.ones((8, 128), F32))
     SC[...] = scale
-    for i in range(6):
-        o_copy(i).wait()
-
-
-def scale_kernel(v_hbm, s_hbm, o_hbm, vin, sin, vout, si, so, ss):
-    def rows(n):
-        return slice(192 * n, 192 * n + 192)
-
-    def come(n):
-        return pltpu.make_async_copy(v_hbm.at[rows(n)], vin.at[rows(n)], si.at[n])
-
+
+
+def scale_kernel(v_ref, s_ref, o_hbm, out, so):
     def go(n):
-        return pltpu.make_async_copy(vout.at[rows(n)], o_hbm.at[rows(n)], so.at[n])
-
-    get_scale = pltpu.make_async_copy(s_hbm, sin, ss)
-    get_scale.start()
+        rows = slice(192 * n, 192 * n + 192)
+        return pltpu.make_async_copy(out.at[rows], o_hbm.at[rows], so.at[n])
+
+    scale = s_ref[0:1, 0:1]
     for n in range(12):
-        come(n).start()
-    get_scale.wait()
-    scale = sin[0:1, 0:1]
-    for n in range(12):
-        come(n).wait()
-        vout[rows(n), :] = (vin[rows(n), :].astype(F32) * scale).astype(BF16)
+        rows = slice(192 * n, 192 * n + 192)
+        out[rows, :] = (v_ref[rows, :] * scale).astype(BF16)
         go(n).start()
     for n in range(12):
         go(n).wait()
@@ -608,11 +586,11 @@
     summed, scale = pl.pallas_call(
         kernel,
         out_shape=(
-            jax.ShapeDtypeStruct((ROWS, LON), BF16),
-            jax.ShapeDtypeStruct((8, 128), F32),
+            pltpu.VMEM((ROWS, LON), F32),
+            pltpu.VMEM((8, 128), F32),
         ),
         in_specs=[hbm] * 9,
-        out_specs=(hbm, vm),
+        out_specs=(vm, vm),
         scratch_shapes=[
             pltpu.VMEM((ROWS, LON), BF16),
             pltpu.VMEM((CHUNKS, 256, LON), BF16),
@@ -623,7 +601,6 @@
             pltpu.VMEM((BAND, 128), F32),
             pltpu.SMEM((2, CHN), F32),
             pltpu.SMEM((2, CHN), F32),
-            pltpu.VMEM((ROWS, LON), F32),
             pltpu.VMEM((ROWS, LON), BF16),
             pltpu.VMEM((CHUNKS, LON, 256), BF16),
             pltpu.VMEM((CHUNKS, 256, LON), BF16),
@@ -658,7 +635,6 @@
             pltpu.VMEM((2, BAND, LON), F32),
             dma((6,)),
             dma((8,)),
-            dma((6,)),
             unit,
             unit,
             unit,
@@ -677,7 +653,7 @@
             dma((N_LAT,)),
         ],
         compiler_params=pltpu.CompilerParams(
-            collective_id=0, has_side_effects=True, vmem_limit_bytes=60 * 1024 * 1024
+            collective_id=0, has_side_effects=True, vmem_limit_bytes=54 * 1024 * 1024
         ),
     )(
         field_in.reshape(ROWS, LON), lon_table(), lat_tables(), mix_first[:, :, 0], mix_bias[:, :, 0],
@@ -686,17 +662,14 @@
     out = pl.pallas_call(
         scale_kernel,
         out_shape=jax.ShapeDtypeStruct((ROWS, LON), BF16),
-        in_specs=[hbm, hbm],
+        in_specs=[vm, vm],
         out_specs=hbm,
-        scratch_shapes=[
-            pltpu.VMEM((ROWS, LON), BF16),
-            pltpu.VMEM((8, 128), F32),
-            pltpu.VMEM((ROWS, LON), BF16),
-            dma((12,)),
-            dma((12,)),
-            dma(()),
-        ],
-    )(summed, scale)
+        scratch_shapes=[pltpu.VMEM((ROWS, LON), BF16), dma((12,))],
+        compiler_params=pltpu.CompilerParams(vmem_limit_bytes=8 * 1024 * 1024),
+    )(
+        pltpu.with_memory_space_constraint(summed, pltpu.VMEM),
+        pltpu.with_memory_space_constraint(scale, pltpu.VMEM),
+    )
     return out.reshape(CHN, BAND, LON)
 
 

time: 202 us -> 200 us (0.990)
  no operation moved by 1% of the time
where the time goes in v4:
time: 200 us
  Pallas kernels  200 us (100%)
    pallas_call x1, Pallas kernels, per_device(): pl.pallas_call(kernel, out_shape=(pltpu.VMEM((ROWS, LON), F32), pltpu.VME...  198 us

profile of v4, /device:TPU:1, one launch (start us, length us, event | category | flops | bytes accessed | tf_op | source)
XLA Modules:
  0.0 199.9 jit_solution(767609477788484181)
XLA Ops:
  0.0 197.9 %shard_map.91 = (f32[2304,768]{1,0:T(8,128)S(1)}, f32[8,128]{1,0:T(8,128)S(1)}) custom-call(bf16[2304,768]{1,0:T(8,128)(2,1)} %bitcast.5, bf16[3,256,768]{2,1,0:T(8,128)(2,1)} %constant.6.clone.tb_hbm, bf16[2,384,384]{2,1,0:T(8,128)(2,1)} %constant.7.clone.cs_hbm, bf16[2,2,96,96]{3,2,1,0:T(8,128)(2,1)} %bitcast.6, bf16[2,2,96]{2,1,0:T(2,128)(2,1)} %bitcast.8, ...), custom_call_target="tpu_custom_call" | custom-call | tf_op jit(solution)/shard_map/pallas_call | solution.py:586
  197.9 2.0 shard_map.92

commit v5 on v4

--- a/solution.py
+++ b/solution.py
@@ -84,10 +84,10 @@
     mc = cx * 2 + ck
 
     def x_copy(i):
-        rows = pl.ds(pl.multiple_of(i * 384, 384), 384)
+        rows = pl.ds(pl.multiple_of(i * 192, 192), 192)
         return pltpu.make_async_copy(x_hbm.at[rows], X.at[rows], xs.at[i])
 
-    for i in range(6):
+    for i in range(12):
         x_copy(i).start()
     small = [
         pltpu.make_async_copy(src, dst, ts.at[n])
@@ -283,7 +283,7 @@
             for q, piece in enumerate(block_swap(parts, masks)):
                 SF[c, u, 8 * half + q, rows_of(ii), :] = piece.astype(BF16)
 
-    def normalize_step(l, srow, i):
+    def normalize_step(l, srow, i, first):
         def pair(j, _):
             base = i * 384 + j * 48
             ch = i * 16 + j * 2
@@ -292,9 +292,14 @@
                 mean = MI[0, :, ls]
                 inv = MI[1, :, ls]
                 both = []
+                if first:
+                    xx = X[pl.ds(pl.multiple_of(base, 48), 48), ls].astype(F32)
                 for t in range(2):
                     rows = pl.ds(pl.multiple_of(base + 24 * t, 24), 24)
-                    cur = (V[rows, ls] * srow).astype(BF16).astype(F32)
+                    if first:
+                        cur = xx[24 * t : 24 * t + 24]
+                    else:
+                        cur = (V[rows, ls] * srow).astype(BF16).astype(F32)
                     nrm = (cur - mean) * inv * gain_ref[l, ch + t] + shift_ref[l, ch + t]
                     nrm = nrm.astype(BF16).astype(F32)
                     V[rows, ls] = cur + nrm
@@ -307,7 +312,14 @@
     def forward_first(l, srow):
         def unit(u, _):
             def step(ii, _):
-                normalize_step(l, srow, u * SUBSTEPS + ii)
+                @pl.when(l == 0)
+                def _():
+                    normalize_step(l, srow, u * SUBSTEPS + ii, True)
+
+                @pl.when(l > 0)
+                def _():
+                    normalize_step(l, srow, u * SUBSTEPS + ii, False)
+
                 forward_step(0, u, ii)
                 return 0
 
@@ -468,33 +480,30 @@
 
         def pair(j, carry):
             s1, s2 = carry
-            rows = pl.ds(pl.multiple_of(i * 384 + j * 48, 48), 48)
+            rows = pl.ds(pl.multiple_of(i * 192 + j * 48, 48), 48)
             xx = X[rows, :].astype(F32)
-            V[rows, :] = xx
             for t in range(2):
                 v = xx[24 * t : 24 * t + 24]
                 s1 = s1 + v
                 s2 = s2 + v * v
             return s1, s2
 
-        return lax.fori_loop(0, 8, pair, carry)
-
-    s1, s2 = lax.fori_loop(0, 6, first_block, (zero, zero))
+        return lax.fori_loop(0, 4, pair, carry)
+
+    s1, s2 = lax.fori_loop(0, 12, first_block, (zero, zero))
     PS[0] = s1
     PS[1] = s2
     small[0].wait()
     stats_out()
     pl.semaphore_wait(bar, len(ORDER) + len(CH_ORDER))
     rs_start()
-    e_start()
     set_tables()
     rs_sum()
     ag_start()
-    EX[1] = e_sum()
+    e_start()
     ag_wait()
     rs_sent()
     ag_sent()
-    e_sent()
 
     def layer(l, scale):
         set_mean_inv(scale)
@@ -502,6 +511,12 @@
         forward_first(l, srow)
         forward_rest()
 
+        @pl.when(l == 0)
+        def _():
+            EX[1] = e_sum()
+            e_sent()
+            row_start(*by_target)
+
         def mid(c, _):
             middle_chunk(l, c)
             return 0
@@ -526,7 +541,6 @@
         def _():
             rs_start()
             e_start()
-            row_start(*by_target)
             rs_sum()
             ag_start()
             EX[0] = e_sum()
@@ -565,15 +579,15 @@
 
 def scale_kernel(v_ref, s_ref, o_hbm, out, so):
     def go(n):
-        rows = slice(192 * n, 192 * n + 192)
+        rows = slice(96 * n, 96 * n + 96)
         return pltpu.make_async_copy(out.at[rows], o_hbm.at[rows], so.at[n])
 
     scale = s_ref[0:1, 0:1]
-    for n in range(12):
-        rows = slice(192 * n, 192 * n + 192)
+    for n in range(24):
+        rows = slice(96 * n, 96 * n + 96)
         out[rows, :] = (v_ref[rows, :] * scale).astype(BF16)
         go(n).start()
-    for n in range(12):
+    for n in range(24):
         go(n).wait()
 
 
@@ -633,7 +647,7 @@
             pltpu.VMEM((8, 128), F32),
             pltpu.VMEM((8, 128), F32),
             pltpu.VMEM((2, BAND, LON), F32),
-            dma((6,)),
+            dma((12,)),
             dma((8,)),
             unit,
             unit,
@@ -664,7 +678,7 @@
         out_shape=jax.ShapeDtypeStruct((ROWS, LON), BF16),
         in_specs=[vm, vm],
         out_specs=hbm,
-        scratch_shapes=[pltpu.VMEM((ROWS, LON), BF16), dma((12,))],
+        scratch_shapes=[pltpu.VMEM((ROWS, LON), BF16), dma((24,))],
         compiler_params=pltpu.CompilerParams(vmem_limit_bytes=8 * 1024 * 1024),
     )(
         pltpu.with_memory_space_constraint(summed, pltpu.VMEM),

time: 200 us -> 200 us (level)
  no operation moved by 1% of the time
where the time goes in v5:
time: 200 us
  Pallas kernels  200 us (100%)
    pallas_call x1, Pallas kernels, per_device(): pl.pallas_call(kernel, out_shape=(pltpu.VMEM((ROWS, LON), F32), pltpu.VME...  198 us

profile of v5, /device:TPU:1, one launch (start us, length us, event | category | flops | bytes accessed | tf_op | source)
XLA Modules:
  0.0 199.6 jit_solution(10446766533459110521)
XLA Ops:
  0.0 197.5 %shard_map.91 = (f32[2304,768]{1,0:T(8,128)S(1)}, f32[8,128]{1,0:T(8,128)S(1)}) custom-call(bf16[2304,768]{1,0:T(8,128)(2,1)} %bitcast.5, bf16[3,256,768]{2,1,0:T(8,128)(2,1)} %constant.6.clone.tb_hbm, bf16[2,384,384]{2,1,0:T(8,128)(2,1)} %constant.7.clone.cs_hbm, bf16[2,2,96,96]{3,2,1,0:T(8,128)(2,1)} %bitcast.6, bf16[2,2,96]{2,1,0:T(2,128)(2,1)} %bitcast.8, ...), custom_call_target="tpu_custom_call" | custom-call | tf_op jit(solution)/shard_map/pallas_call | solution.py:600
  197.6 2.0 %shard_map.92 = bf16[2304,768]{1,0:T(8,128)(2,1)} custom-call(f32[2304,768]{1,0:T(8,128)S(1)} %get-tuple-element.7.v_ref, f32[8,128]{1,0:T(8,128)S(1)} %get-tuple-element.8.s_ref), custom_call_target="tpu_custom_call" | custom-call | tf_op jit(solution)/shard_map/pallas_call | solution.py:676
